TPU v7x, 8 devices: a whole 2x2x1 slice. The times are simulated.
8 devices in a mesh: col: 2 (over z, y), row: 4 (over x, core).
Axes of the slice: x: 2, y: 2, z: 1, core: 2. Of those that a mesh axis runs over, the one named last changes fastest.
Arguments:
- forcing: float32 [2, 192, 96, 256], P(None, 'row', 'col')
- init_guess: float32 [2, 192, 96, 256], P(None, 'row', 'col')
- cell_coef: float32 [2, 192, 96], P(None, 'row', 'col')
- solve_rows: bfloat16 [2, 4, 2, 2304, 4096], P(None, 'row', 'col')
- relax_factor: float32 [2], replicated
Outputs:
- output: float32 [2, 192, 96, 256], P(None, 'row', 'col')
All inputs are finite; a program needn't handle non-finite values.
Results may differ from a plain program's by a relative error of at most 0.00124.
Values are sent between devices in bfloat16 or wider.
A program may use at most 1 GiB of HBM per device.

v0:
```python
import math
import jax
import jax.numpy as jnp
from jax import lax
from jax.sharding import PartitionSpec as P

SWEEPS = 4


def up_perm(axis_size):
    return [(device, device + 1) for device in range(axis_size - 1)]


def down_perm(axis_size):
    return [(device + 1, device) for device in range(axis_size - 1)]


def grow_halo(values, halo_width, grid_dim, axis_name, axis_size):
    extent = values.shape[grid_dim]
    low_edge = lax.slice_in_dim(values, 0, halo_width, axis=grid_dim)
    high_edge = lax.slice_in_dim(values, extent - halo_width, extent, axis=grid_dim)
    from_below = lax.ppermute(high_edge, axis_name, up_perm(axis_size))
    from_above = lax.ppermute(low_edge, axis_name, down_perm(axis_size))
    return jnp.concatenate([from_below, values, from_above], axis=grid_dim)


def edge_faces(coef_grid, grid_dim, axis_name, axis_size):
    position = lax.axis_index(axis_name)
    extent = coef_grid.shape[grid_dim]
    low_edge = lax.slice_in_dim(coef_grid, 0, 1, axis=grid_dim)
    high_edge = lax.slice_in_dim(coef_grid, extent - 1, extent, axis=grid_dim)
    from_below = lax.ppermute(high_edge, axis_name, up_perm(axis_size))
    from_above = lax.ppermute(low_edge, axis_name, down_perm(axis_size))
    low_side = jnp.where(position == 0, low_edge, from_below)
    high_side = jnp.where(position == axis_size - 1, high_edge, from_above)
    widened = jnp.concatenate([low_side, coef_grid, high_side], axis=grid_dim)
    return 0.5 * (lax.slice_in_dim(widened, 0, extent + 1, axis=grid_dim) + lax.slice_in_dim(widened, 1, extent + 2, axis=grid_dim))


def apply_local(face_x, face_y, wide_x, wide_y):
    flux_x = face_x[..., None] * (wide_x[:, 1:] - wide_x[:, :-1])
    flux_y = face_y[..., None] * (wide_y[:, :, 1:] - wide_y[:, :, :-1])
    return flux_x[:, :-1] - flux_x[:, 1:] + flux_y[:, :, :-1] - flux_y[:, :, 1:]


def solution(mesh):
    row_count = mesh.shape["row"]
    col_count = mesh.shape["col"]
    grid_spec = P(None, "row", "col", None)

    def local_sweeps(forcing, init_guess, cell_coef, solve_rows, relax_factor):
        num_sys, sub_size, _, num_rhs = forcing.shape
        ext_size = math.isqrt(solve_rows.shape[-1])
        margin = (ext_size - sub_size) // 2
        solve_mat = solve_rows.reshape(num_sys, sub_size * sub_size, ext_size * ext_size)
        step_size = relax_factor[:, None, None, None]
        face_x = edge_faces(cell_coef, 1, "row", row_count)
        face_y = edge_faces(cell_coef, 2, "col", col_count)

        def apply_op(values):
            return apply_local(face_x, face_y, grow_halo(values, 1, 1, "row", row_count), grow_halo(values, 1, 2, "col", col_count))

        residual = forcing - apply_op(init_guess)
        approx = init_guess
        for _ in range(SWEEPS):
            low_res = residual.astype(jnp.bfloat16)
            window = grow_halo(grow_halo(low_res, margin, 1, "row", row_count), margin, 2, "col", col_count)
            correction = jnp.einsum("sqe,sek->sqk", solve_mat, window.reshape(num_sys, ext_size * ext_size, num_rhs), preferred_element_type=jnp.float32)
            correction = correction.reshape(num_sys, sub_size, sub_size, num_rhs)
            approx = approx + step_size * correction
            residual = residual - step_size * apply_op(correction)
        return approx

    return jax.shard_map(local_sweeps, mesh=mesh, in_specs=(grid_spec, grid_spec, P(None, "row", "col"), P(None, "row", "col", None, None), P(None)), out_specs=grid_spec, check_vma=False)
```

profile of v0, /device:TPU:1, one launch (start us, length us, event | category | flops | bytes accessed | tf_op | source)
XLA Modules:
  0.0 334.3 jit_solution(5034573246747229987)
XLA Ops:
  0.7 1.9 collective-permute-start.1
  2.6 4.5 %collective-permute-start = (f32[2,1,48]{2,1,0:T(1,128)S(1)}, f32[2,1,48]{2,1,0:T(1,128)S(1)}, u32[]{:S(2)}, u32[]{:S(2)}) collective-permute-start(f32[2,1,48]{2,1,0:T(1,128)S(1)} %get-tuple-element.46), channel_id=1, source_target_pairs={{0,1},{1,2},{2,3},{4,5},{5,6},{6,7}} | collective-permute-start | bytes 1160 | tf_op jit(solution)/shard_map/ppermute | solution.py:32
  9.4 4.0 %collective-permute-start.4 = (f32[2,48,1]{2,1,0:T(8,128)S(1)}, f32[2,48,1]{2,1,0:T(8,128)S(1)}, u32[]{:S(2)}, u32[]{:S(2)}) collective-permute-start(f32[2,48,1]{2,1,0:T(8,128)S(1)} %get-tuple-element.50), channel_id=1, source_target_pairs={{0,4},{1,5},{2,6},{3,7}} | collective-permute-start | bytes 1160 | tf_op jit(solution)/shard_map/ppermute | solution.py:32
  14.4 3.0 collective-permute-start.3
  18.9 1.9 collective-permute-start.2
  27.1 4.6 %fusion.24 = f32[2,49,48,256]{3,2,1,0:T(8,128)S(1)} fusion(f32[2,1,48,256]{3,2,1,0:T(8,128)S(1)} %collective-permute-done.2, f32[2,48,48,256]{3,2,1,0:T(8,128)} %param.6, f32[2,1,48,256]{3,2,1,0:T(8,128)S(1)} %collective-permute-done.3, f32[2,49,48]{2,1,0:T(8,128)S(1)} %fusion.36), kind=kLoop, calls=%fused_computation.21 | loop fusion | flops 4816896 | bytes 9750912 | tf_op jit(solution)/shard_map/mul | solution.py:41
  33.3 3.9 %fusion.42 = (bf16[2,48,48,256]{3,2,1,0:T(8,128)(2,1)S(1)}, f32[2,48,48,256]{3,2,1,0:T(8,128)}) fusion(f32[2,48,48,256]{3,2,1,0:T(8,128)S(1)} %bitcast.68, f32[2,48,49,256]{3,2,1,0:T(8,128)S(1)} %fusion.8, f32[2,49,48,256]{3,2,1,0:T(8,128)S(1)} %fusion.24), kind=kLoop, calls=%fused_computation.75 | loop fusion | flops 5898240 | bytes 30670848 | tf_op jit(solution)/shard_map/convert_element_type | solution.py:66
  37.3 3.6 %collective-permute-start.8 = (bf16[2,8,48,256]{3,2,1,0:T(8,128)(2,1)S(1)}, bf16[2,8,48,256]{3,2,1,0:T(8,128)(2,1)S(1)}, u32[]{:S(2)}, u32[]{:S(2)}) collective-permute-start(bf16[2,8,48,256]{3,2,1,0:T(8,128)(2,1)S(1)} %get-tuple-element.41), channel_id=1, source_target_pairs={{0,1},{1,2},{2,3},{4,5},{5,6},{6,7}} | collective-permute-start | bytes 1179656 | tf_op jit(solution)/shard_map/ppermute | solution.py:22
  40.9 1.9 collective-permute-start.9
  42.9 2.8 collective-permute-done.8
  45.6 4.4 %collective-permute-done.9 = bf16[2,8,48,256]{3,2,1,0:T(8,128)(2,1)S(1)} collective-permute-done((bf16[2,8,48,256]{3,2,1,0:T(8,128)(2,1)S(1)}, bf16[2,8,48,256]{3,2,1,0:T(8,128)(2,1)S(1)}, u32[]{:S(2)}, u32[]{:S(2)}) %collective-permute-start.9) | collective-permute-done | bytes 393248 | tf_op jit(solution)/shard_map/ppermute | solution.py:23
  50.1 4.6 %collective-permute-start.10 = (bf16[2,64,8,256]{3,2,1,0:T(8,128)(2,1)S(1)}, bf16[2,64,8,256]{3,2,1,0:T(8,128)(2,1)S(1)}, u32[]{:S(2)}, u32[]{:S(2)}) collective-permute-start(bf16[2,64,8,256]{3,2,1,0:T(8,128)(2,1)S(1)} %get-tuple-element.33), channel_id=1, source_target_pairs={{0,4},{1,5},{2,6},{3,7}} | collective-permute-start | bytes 1572872 | tf_op jit(solution)/shard_map/ppermute | solution.py:22
  56.0 5.1 %collective-permute-done.10 = bf16[2,64,8,256]{3,2,1,0:T(8,128)(2,1)S(1)} collective-permute-done((bf16[2,64,8,256]{3,2,1,0:T(8,128)(2,1)S(1)}, bf16[2,64,8,256]{3,2,1,0:T(8,128)(2,1)S(1)}, u32[]{:S(2)}, u32[]{:S(2)}) %collective-permute-start.10) | collective-permute-done | bytes 524320 | tf_op jit(solution)/shard_map/ppermute | solution.py:22
  61.1 4.2 %collective-permute-done.11 = bf16[2,64,8,256]{3,2,1,0:T(8,128)(2,1)S(1)} collective-permute-done((bf16[2,64,8,256]{3,2,1,0:T(8,128)(2,1)S(1)}, bf16[2,64,8,256]{3,2,1,0:T(8,128)(2,1)S(1)}, u32[]{:S(2)}, u32[]{:S(2)}) %collective-permute-start.11) | collective-permute-done | bytes 524320 | tf_op jit(solution)/shard_map/ppermute | solution.py:23
  65.2 2.3 pad_maximum_fusion
  67.5 20.2 %fusion.12 = f32[2,2304,256]{1,2,0:T(8,128)} fusion(bf16[2,4096,256]{2,1,0:T(8,128)(2,1)} %bitcast.69, bf16[2,1,1,2304,4096]{4,3,2,1,0:T(8,128)(2,1)} %param.8), kind=kOutput, calls=%fused_computation.16 | convolution fusion | flops 9663676416 | bytes 46661632 | tf_op jit(solution)/shard_map/sqe,sek->sqk/dot_general | solution.py:68
  87.7 6.1 %copy.39 = f32[2,2304,256]{2,1,0:T(8,128)} copy(f32[2,2304,256]{1,2,0:T(8,128)} %fusion.12) | data formatting | bytes 9437184 | tf_op jit(solution)/shard_map/sqe,sek->sqk/dot_general | solution.py:68
  94.8 2.3 collective-permute-start.13
  97.0 2.1 collective-permute-start.12
  102.1 1.6 collective-permute-start.14
  103.7 4.4 %fusion.25 = f32[2,49,48,256]{3,2,1,0:T(8,128)S(1)} fusion(f32[2,1,48,256]{3,2,1,0:T(8,128)S(1)} %collective-permute-done.12, f32[2,48,48,256]{3,2,1,0:T(8,128)} %bitcast.39, f32[2,1,48,256]{3,2,1,0:T(8,128)S(1)} %collective-permute-done.13, f32[2,49,48]{2,1,0:T(8,128)S(1)} %fusion.36), kind=kLoop, calls=%fused_computation.23 | loop fusion | flops 4816896 | bytes 9750912 | tf_op jit(solution)/shard_map/mul | solution.py:41
  110.4 3.9 %fusion.40 = (bf16[2,48,48,256]{3,2,1,0:T(8,128)(2,1)S(1)}, f32[2,48,48,256]{3,2,1,0:T(8,128)}) fusion(f32[2,48,48,256]{3,2,1,0:T(8,128)S(1)} %bitcast.66, f32[2,48,49,256]{3,2,1,0:T(8,128)S(1)} %fusion.9, f32[2,49,48,256]{3,2,1,0:T(8,128)S(1)} %fusion.25, f32[2]{0:T(128)S(1)} %copy-done), kind=kLoop, calls=%fused_computation.74 | loop fusion | flops 7077888 | bytes 30670856 | tf_op jit(solution)/shard_map/convert_element_type | solution.py:66
  114.4 3.4 %collective-permute-start.16 = (bf16[2,8,48,256]{3,2,1,0:T(8,128)(2,1)S(1)}, bf16[2,8,48,256]{3,2,1,0:T(8,128)(2,1)S(1)}, u32[]{:S(2)}, u32[]{:S(2)}) collective-permute-start(bf16[2,8,48,256]{3,2,1,0:T(8,128)(2,1)S(1)} %get-tuple-element.39), channel_id=1, source_target_pairs={{0,1},{1,2},{2,3},{4,5},{5,6},{6,7}} | collective-permute-start | bytes 1179656 | tf_op jit(solution)/shard_map/ppermute | solution.py:22
  117.8 1.9 collective-permute-start.17
  119.8 2.8 collective-permute-done.16
  122.5 4.4 %collective-permute-done.17 = bf16[2,8,48,256]{3,2,1,0:T(8,128)(2,1)S(1)} collective-permute-done((bf16[2,8,48,256]{3,2,1,0:T(8,128)(2,1)S(1)}, bf16[2,8,48,256]{3,2,1,0:T(8,128)(2,1)S(1)}, u32[]{:S(2)}, u32[]{:S(2)}) %collective-permute-start.17) | collective-permute-done | bytes 393248 | tf_op jit(solution)/shard_map/ppermute | solution.py:23
  127.0 3.9 %collective-permute-start.18 = (bf16[2,64,8,256]{3,2,1,0:T(8,128)(2,1)S(1)}, bf16[2,64,8,256]{3,2,1,0:T(8,128)(2,1)S(1)}, u32[]{:S(2)}, u32[]{:S(2)}) collective-permute-start(bf16[2,64,8,256]{3,2,1,0:T(8,128)(2,1)S(1)} %get-tuple-element.31), channel_id=1, source_target_pairs={{0,4},{1,5},{2,6},{3,7}} | collective-permute-start | bytes 1572872 | tf_op jit(solution)/shard_map/ppermute | solution.py:22
  132.4 4.9 %collective-permute-done.18 = bf16[2,64,8,256]{3,2,1,0:T(8,128)(2,1)S(1)} collective-permute-done((bf16[2,64,8,256]{3,2,1,0:T(8,128)(2,1)S(1)}, bf16[2,64,8,256]{3,2,1,0:T(8,128)(2,1)S(1)}, u32[]{:S(2)}, u32[]{:S(2)}) %collective-permute-start.18) | collective-permute-done | bytes 524320 | tf_op jit(solution)/shard_map/ppermute | solution.py:22
  137.3 4.2 %collective-permute-done.19 = bf16[2,64,8,256]{3,2,1,0:T(8,128)(2,1)S(1)} collective-permute-done((bf16[2,64,8,256]{3,2,1,0:T(8,128)(2,1)S(1)}, bf16[2,64,8,256]{3,2,1,0:T(8,128)(2,1)S(1)}, u32[]{:S(2)}, u32[]{:S(2)}) %collective-permute-start.19) | collective-permute-done | bytes 524320 | tf_op jit(solution)/shard_map/ppermute | solution.py:23
  141.4 2.3 pad_maximum_fusion.1
  143.7 20.2 %fusion.15 = f32[2,2304,256]{1,2,0:T(8,128)} fusion(bf16[2,4096,256]{2,1,0:T(8,128)(2,1)} %bitcast.70, bf16[2,1,1,2304,4096]{4,3,2,1,0:T(8,128)(2,1)} %param.8), kind=kOutput, calls=%fused_computation.17 | convolution fusion | flops 9663676416 | bytes 46661632 | tf_op jit(solution)/shard_map/sqe,sek->sqk/dot_general | solution.py:68
  163.9 6.1 %copy.41 = f32[2,2304,256]{2,1,0:T(8,128)} copy(f32[2,2304,256]{1,2,0:T(8,128)} %fusion.15) | data formatting | bytes 9437184 | tf_op jit(solution)/shard_map/sqe,sek->sqk/dot_general | solution.py:68
  171.0 2.3 collective-permute-start.21
  173.2 2.1 collective-permute-start.20
  178.3 1.6 collective-permute-start.22
  179.9 4.5 %fusion.26 = f32[2,49,48,256]{3,2,1,0:T(8,128)S(1)} fusion(f32[2,1,48,256]{3,2,1,0:T(8,128)S(1)} %collective-permute-done.20, f32[2,48,48,256]{3,2,1,0:T(8,128)} %bitcast.46, f32[2,1,48,256]{3,2,1,0:T(8,128)S(1)} %collective-permute-done.21, f32[2,49,48]{2,1,0:T(8,128)S(1)} %fusion.36), kind=kLoop, calls=%fused_computation.25 | loop fusion | flops 4816896 | bytes 9750912 | tf_op jit(solution)/shard_map/mul | solution.py:41
  186.6 3.9 %fusion.38 = (bf16[2,48,48,256]{3,2,1,0:T(8,128)(2,1)S(1)}, f32[2,48,48,256]{3,2,1,0:T(8,128)}) fusion(f32[2,48,48,256]{3,2,1,0:T(8,128)S(1)} %bitcast.61, f32[2,48,49,256]{3,2,1,0:T(8,128)S(1)} %fusion.10, f32[2,49,48,256]{3,2,1,0:T(8,128)S(1)} %fusion.26, f32[2]{0:T(128)S(1)} %copy-done), kind=kLoop, calls=%fused_computation.73 | loop fusion | flops 7077888 | bytes 30670856 | tf_op jit(solution)/shard_map/convert_element_type | solution.py:66
  190.6 3.4 %collective-permute-start.24 = (bf16[2,8,48,256]{3,2,1,0:T(8,128)(2,1)S(1)}, bf16[2,8,48,256]{3,2,1,0:T(8,128)(2,1)S(1)}, u32[]{:S(2)}, u32[]{:S(2)}) collective-permute-start(bf16[2,8,48,256]{3,2,1,0:T(8,128)(2,1)S(1)} %get-tuple-element.37), channel_id=1, source_target_pairs={{0,1},{1,2},{2,3},{4,5},{5,6},{6,7}} | collective-permute-start | bytes 1179656 | tf_op jit(solution)/shard_map/ppermute | solution.py:22
  194.0 1.9 collective-permute-start.25
  195.9 2.8 collective-permute-done.24
  198.7 4.4 %collective-permute-done.25 = bf16[2,8,48,256]{3,2,1,0:T(8,128)(2,1)S(1)} collective-permute-done((bf16[2,8,48,256]{3,2,1,0:T(8,128)(2,1)S(1)}, bf16[2,8,48,256]{3,2,1,0:T(8,128)(2,1)S(1)}, u32[]{:S(2)}, u32[]{:S(2)}) %collective-permute-start.25) | collective-permute-done | bytes 393248 | tf_op jit(solution)/shard_map/ppermute | solution.py:23
  203.2 4.0 %collective-permute-start.26 = (bf16[2,64,8,256]{3,2,1,0:T(8,128)(2,1)S(1)}, bf16[2,64,8,256]{3,2,1,0:T(8,128)(2,1)S(1)}, u32[]{:S(2)}, u32[]{:S(2)}) collective-permute-start(bf16[2,64,8,256]{3,2,1,0:T(8,128)(2,1)S(1)} %get-tuple-element.29), channel_id=1, source_target_pairs={{0,4},{1,5},{2,6},{3,7}} | collective-permute-start | bytes 1572872 | tf_op jit(solution)/shard_map/ppermute | solution.py:22
  208.7 4.8 %collective-permute-done.26 = bf16[2,64,8,256]{3,2,1,0:T(8,128)(2,1)S(1)} collective-permute-done((bf16[2,64,8,256]{3,2,1,0:T(8,128)(2,1)S(1)}, bf16[2,64,8,256]{3,2,1,0:T(8,128)(2,1)S(1)}, u32[]{:S(2)}, u32[]{:S(2)}) %collective-permute-start.26) | collective-permute-done | bytes 524320 | tf_op jit(solution)/shard_map/ppermute | solution.py:22
  213.6 4.2 %collective-permute-done.27 = bf16[2,64,8,256]{3,2,1,0:T(8,128)(2,1)S(1)} collective-permute-done((bf16[2,64,8,256]{3,2,1,0:T(8,128)(2,1)S(1)}, bf16[2,64,8,256]{3,2,1,0:T(8,128)(2,1)S(1)}, u32[]{:S(2)}, u32[]{:S(2)}) %collective-permute-start.27) | collective-permute-done | bytes 524320 | tf_op jit(solution)/shard_map/ppermute | solution.py:23
  217.7 2.3 pad_maximum_fusion.2
  220.1 20.2 %fusion.18 = f32[2,2304,256]{1,2,0:T(8,128)} fusion(bf16[2,4096,256]{2,1,0:T(8,128)(2,1)} %bitcast.71, bf16[2,1,1,2304,4096]{4,3,2,1,0:T(8,128)(2,1)} %param.8), kind=kOutput, calls=%fused_computation.18 | convolution fusion | flops 9663676416 | bytes 46661632 | tf_op jit(solution)/shard_map/sqe,sek->sqk/dot_general | solution.py:68
  240.3 6.1 %copy.43 = f32[2,2304,256]{2,1,0:T(8,128)} copy(f32[2,2304,256]{1,2,0:T(8,128)} %fusion.18) | data formatting | bytes 9437184 | tf_op jit(solution)/shard_map/sqe,sek->sqk/dot_general | solution.py:68
  247.3 2.3 collective-permute-start.29
  249.6 2.1 collective-permute-start.28
  254.6 1.6 collective-permute-start.30
  256.2 4.6 %fusion.27 = f32[2,49,48,256]{3,2,1,0:T(8,128)S(1)} fusion(f32[2,1,48,256]{3,2,1,0:T(8,128)S(1)} %collective-permute-done.28, f32[2,48,48,256]{3,2,1,0:T(8,128)} %bitcast.53, f32[2,1,48,256]{3,2,1,0:T(8,128)S(1)} %collective-permute-done.29, f32[2,49,48]{2,1,0:T(8,128)S(1)} %fusion.36), kind=kLoop, calls=%fused_computation.27 | loop fusion | flops 4816896 | bytes 9750912 | tf_op jit(solution)/shard_map/mul | solution.py:41
  262.9 2.6 fusion.30
  265.7 3.4 %collective-permute-start.32 = (bf16[2,8,48,256]{3,2,1,0:T(8,128)(2,1)S(1)}, bf16[2,8,48,256]{3,2,1,0:T(8,128)(2,1)S(1)}, u32[]{:S(2)}, u32[]{:S(2)}) collective-permute-start(bf16[2,8,48,256]{3,2,1,0:T(8,128)(2,1)S(1)} %get-tuple-element.35), channel_id=1, source_target_pairs={{0,1},{1,2},{2,3},{4,5},{5,6},{6,7}} | collective-permute-start | bytes 1179656 | tf_op jit(solution)/shard_map/ppermute | solution.py:22
  269.1 1.9 collective-permute-start.33
  271.0 2.8 collective-permute-done.32
  273.8 4.4 %collective-permute-done.33 = bf16[2,8,48,256]{3,2,1,0:T(8,128)(2,1)S(1)} collective-permute-done((bf16[2,8,48,256]{3,2,1,0:T(8,128)(2,1)S(1)}, bf16[2,8,48,256]{3,2,1,0:T(8,128)(2,1)S(1)}, u32[]{:S(2)}, u32[]{:S(2)}) %collective-permute-start.33) | collective-permute-done | bytes 393248 | tf_op jit(solution)/shard_map/ppermute | solution.py:23
  278.3 4.1 %collective-permute-start.34 = (bf16[2,64,8,256]{3,2,1,0:T(8,128)(2,1)S(1)}, bf16[2,64,8,256]{3,2,1,0:T(8,128)(2,1)S(1)}, u32[]{:S(2)}, u32[]{:S(2)}) collective-permute-start(bf16[2,64,8,256]{3,2,1,0:T(8,128)(2,1)S(1)} %get-tuple-element.27), channel_id=1, source_target_pairs={{0,4},{1,5},{2,6},{3,7}} | collective-permute-start | bytes 1572872 | tf_op jit(solution)/shard_map/ppermute | solution.py:22
  282.3 1.6 collective-permute-start.35
  283.9 4.8 %collective-permute-done.34 = bf16[2,64,8,256]{3,2,1,0:T(8,128)(2,1)S(1)} collective-permute-done((bf16[2,64,8,256]{3,2,1,0:T(8,128)(2,1)S(1)}, bf16[2,64,8,256]{3,2,1,0:T(8,128)(2,1)S(1)}, u32[]{:S(2)}, u32[]{:S(2)}) %collective-permute-start.34) | collective-permute-done | bytes 524320 | tf_op jit(solution)/shard_map/ppermute | solution.py:22
  288.7 4.2 %collective-permute-done.35 = bf16[2,64,8,256]{3,2,1,0:T(8,128)(2,1)S(1)} collective-permute-done((bf16[2,64,8,256]{3,2,1,0:T(8,128)(2,1)S(1)}, bf16[2,64,8,256]{3,2,1,0:T(8,128)(2,1)S(1)}, u32[]{:S(2)}, u32[]{:S(2)}) %collective-permute-start.35) | collective-permute-done | bytes 524320 | tf_op jit(solution)/shard_map/ppermute | solution.py:23
  292.9 2.2 pad_maximum_fusion.3
  295.1 20.2 %fusion.21 = f32[2,2304,256]{1,2,0:T(8,128)} fusion(bf16[2,4096,256]{2,1,0:T(8,128)(2,1)} %bitcast.72, bf16[2,1,1,2304,4096]{4,3,2,1,0:T(8,128)(2,1)} %param.8), kind=kOutput, calls=%fused_computation.19 | convolution fusion | flops 9663676416 | bytes 46661632 | tf_op jit(solution)/shard_map/sqe,sek->sqk/dot_general | solution.py:68
  315.3 6.1 %copy.45 = f32[2,2304,256]{2,1,0:T(8,128)} copy(f32[2,2304,256]{1,2,0:T(8,128)} %fusion.21) | data formatting | bytes 9437184 | tf_op jit(solution)/shard_map/sqe,sek->sqk/dot_general | solution.py:68
  321.4 12.9 %multiply_add_fusion = f32[2,48,48,256]{3,2,1,0:T(8,128)} fusion(f32[2,48,48,256]{3,2,1,0:T(8,128)} %bitcast.64, f32[2,48,48,256]{3,2,1,0:T(8,128)} %bitcast.54, f32[2,48,48,256]{3,2,1,0:T(8,128)} %bitcast.47, f32[2,48,48,256]{3,2,1,0:T(8,128)} %param.6, f32[2,48,48,256]{3,2,1,0:T(8,128)} %bitcast.40, f32[2]{0:T(128)S(1)} %copy-done), kind=kLoop, calls=%fused_computation.48 | loop fusion | flops 9437184 | bytes 28311560 | tf_op jit(solution)/shard_map/add | solution.py:70
  (97 shorter events, 36.2 us)
Async XLA Ops:
  0.7 18.1 %collective-permute-start.1 = (f32[2,1,48]{2,1,0:T(1,128)S(1)}, f32[2,1,48]{2,1,0:T(1,128)S(1)}, u32[]{:S(2)}, u32[]{:S(2)}) collective-permute-start(f32[2,1,48]{2,1,0:T(1,128)S(1)} %get-tuple-element.45), channel_id=1, source_target_pairs={{1,0},{2,1},{3,2},{5,4},{6,5},{7,6}} | collective-permute-start | bytes 1160 | tf_op jit(solution)/shard_map/ppermute | solution.py:33
  2.6 18.2 %collective-permute-start = (f32[2,1,48]{2,1,0:T(1,128)S(1)}, f32[2,1,48]{2,1,0:T(1,128)S(1)}, u32[]{:S(2)}, u32[]{:S(2)}) collective-permute-start(f32[2,1,48]{2,1,0:T(1,128)S(1)} %get-tuple-element.46), channel_id=1, source_target_pairs={{0,1},{1,2},{2,3},{4,5},{5,6},{6,7}} | collective-permute-start | bytes 1160 | tf_op jit(solution)/shard_map/ppermute | solution.py:32
  8.1 15.6 %collective-permute-start.5 = (f32[2,48,1]{2,1,0:T(8,128)S(1)}, f32[2,48,1]{2,1,0:T(8,128)S(1)}, u32[]{:S(2)}, u32[]{:S(2)}) collective-permute-start(f32[2,48,1]{2,1,0:T(8,128)S(1)} %get-tuple-element.49), channel_id=1, source_target_pairs={{4,0},{5,1},{6,2},{7,3}} | collective-permute-start | bytes 1160 | tf_op jit(solution)/shard_map/ppermute | solution.py:33
  9.4 15.7 %collective-permute-start.4 = (f32[2,48,1]{2,1,0:T(8,128)S(1)}, f32[2,48,1]{2,1,0:T(8,128)S(1)}, u32[]{:S(2)}, u32[]{:S(2)}) collective-permute-start(f32[2,48,1]{2,1,0:T(8,128)S(1)} %get-tuple-element.50), channel_id=1, source_target_pairs={{0,4},{1,5},{2,6},{3,7}} | collective-permute-start | bytes 1160 | tf_op jit(solution)/shard_map/ppermute | solution.py:32
  14.4 12.8 %collective-permute-start.3 = (f32[2,1,48,256]{3,2,1,0:T(8,128)S(1)}, f32[2,1,48,256]{3,2,1,0:T(8,128)S(1)}, u32[]{:S(2)}, u32[]{:S(2)}) collective-permute-start(f32[2,1,48,256]{3,2,1,0:T(8,128)S(1)} %get-tuple-element.23), channel_id=1, source_target_pairs={{0,1},{1,2},{2,3},{4,5},{5,6},{6,7}} | collective-permute-start | bytes 294920 | tf_op jit(solution)/shard_map/ppermute | solution.py:22
  18.9 8.3 %collective-permute-start.2 = (f32[2,1,48,256]{3,2,1,0:T(8,128)S(1)}, f32[2,1,48,256]{3,2,1,0:T(8,128)S(1)}, u32[]{:S(2)}, u32[]{:S(2)}) collective-permute-start(f32[2,1,48,256]{3,2,1,0:T(8,128)S(1)} %get-tuple-element.24), channel_id=1, source_target_pairs={{1,0},{2,1},{3,2},{5,4},{6,5},{7,6}} | collective-permute-start | bytes 294920 | tf_op jit(solution)/shard_map/ppermute | solution.py:23
  20.8 10.9 %collective-permute-start.7 = (f32[2,48,1,256]{3,2,1,0:T(1,128)S(1)}, f32[2,48,1,256]{3,2,1,0:T(1,128)S(1)}, u32[]{:S(2)}, u32[]{:S(2)}) collective-permute-start(f32[2,48,1,256]{3,2,1,0:T(1,128)S(1)} %get-tuple-element.25), channel_id=1, source_target_pairs={{0,4},{1,5},{2,6},{3,7}} | collective-permute-start | bytes 294920 | tf_op jit(solution)/shard_map/ppermute | solution.py:22
  23.7 8.0 %collective-permute-start.6 = (f32[2,48,1,256]{3,2,1,0:T(1,128)S(1)}, f32[2,48,1,256]{3,2,1,0:T(1,128)S(1)}, u32[]{:S(2)}, u32[]{:S(2)}) collective-permute-start(f32[2,48,1,256]{3,2,1,0:T(1,128)S(1)} %get-tuple-element.26), channel_id=1, source_target_pairs={{4,0},{5,1},{6,2},{7,3}} | collective-permute-start | bytes 294920 | tf_op jit(solution)/shard_map/ppermute | solution.py:23
  26.0 5.8 %slice-start.6 = ((s8[4718592]{0:T(1024)(128)(4,1)}), s8[4194304]{0:T(1024)(128)(4,1)S(1)}, s32[]{:S(2)}) async-start(s8[4718592]{0:T(1024)(128)(4,1)} %bitcast.58), calls=%async_computation.6 | async-start | bytes 8388608
  27.1 4.7 %slice-start.7 = ((s8[4718592]{0:T(1024)(128)(4,1)}), s8[524288]{0:T(1024)(128)(4,1)S(1)}, s32[]{:S(2)}) async-start(s8[4718592]{0:T(1024)(128)(4,1)} %bitcast.58), calls=%async_computation.7 | async-start | bytes 1048576
  27.1 6.1 %slice-start.14 = ((s8[4718592]{0:T(1024)(128)(4,1)}), s8[4194304]{0:T(1024)(128)(4,1)S(1)}, s32[]{:S(2)}) async-start(s8[4718592]{0:T(1024)(128)(4,1)} %bitcast.67), calls=%async_computation.14 | async-start | bytes 8388608
  31.7 1.5 slice-start.15
  37.3 8.3 %collective-permute-start.8 = (bf16[2,8,48,256]{3,2,1,0:T(8,128)(2,1)S(1)}, bf16[2,8,48,256]{3,2,1,0:T(8,128)(2,1)S(1)}, u32[]{:S(2)}, u32[]{:S(2)}) collective-permute-start(bf16[2,8,48,256]{3,2,1,0:T(8,128)(2,1)S(1)} %get-tuple-element.41), channel_id=1, source_target_pairs={{0,1},{1,2},{2,3},{4,5},{5,6},{6,7}} | collective-permute-start | bytes 1179656 | tf_op jit(solution)/shard_map/ppermute | solution.py:22
  40.9 9.1 %collective-permute-start.9 = (bf16[2,8,48,256]{3,2,1,0:T(8,128)(2,1)S(1)}, bf16[2,8,48,256]{3,2,1,0:T(8,128)(2,1)S(1)}, u32[]{:S(2)}, u32[]{:S(2)}) collective-permute-start(bf16[2,8,48,256]{3,2,1,0:T(8,128)(2,1)S(1)} %get-tuple-element.42), channel_id=1, source_target_pairs={{1,0},{2,1},{3,2},{5,4},{6,5},{7,6}} | collective-permute-start | bytes 1179656 | tf_op jit(solution)/shard_map/ppermute | solution.py:23
  50.1 11.0 %collective-permute-start.10 = (bf16[2,64,8,256]{3,2,1,0:T(8,128)(2,1)S(1)}, bf16[2,64,8,256]{3,2,1,0:T(8,128)(2,1)S(1)}, u32[]{:S(2)}, u32[]{:S(2)}) collective-permute-start(bf16[2,64,8,256]{3,2,1,0:T(8,128)(2,1)S(1)} %get-tuple-element.33), channel_id=1, source_target_pairs={{0,4},{1,5},{2,6},{3,7}} | collective-permute-start | bytes 1572872 | tf_op jit(solution)/shard_map/ppermute | solution.py:22
  54.7 10.5 %collective-permute-start.11 = (bf16[2,64,8,256]{3,2,1,0:T(8,128)(2,1)S(1)}, bf16[2,64,8,256]{3,2,1,0:T(8,128)(2,1)S(1)}, u32[]{:S(2)}, u32[]{:S(2)}) collective-permute-start(bf16[2,64,8,256]{3,2,1,0:T(8,128)(2,1)S(1)} %get-tuple-element.34), channel_id=1, source_target_pairs={{4,0},{5,1},{6,2},{7,3}} | collective-permute-start | bytes 1572872 | tf_op jit(solution)/shard_map/ppermute | solution.py:23
  94.8 8.9 %collective-permute-start.13 = (f32[2,1,48,256]{3,2,1,0:T(8,128)S(1)}, f32[2,1,48,256]{3,2,1,0:T(8,128)S(1)}, u32[]{:S(2)}, u32[]{:S(2)}) collective-permute-start(f32[2,1,48,256]{3,2,1,0:T(8,128)S(1)} %get-tuple-element.19), channel_id=1, source_target_pairs={{0,1},{1,2},{2,3},{4,5},{5,6},{6,7}} | collective-permute-start | bytes 294920 | tf_op jit(solution)/shard_map/ppermute | solution.py:22
  97.0 6.6 %collective-permute-start.12 = (f32[2,1,48,256]{3,2,1,0:T(8,128)S(1)}, f32[2,1,48,256]{3,2,1,0:T(8,128)S(1)}, u32[]{:S(2)}, u32[]{:S(2)}) collective-permute-start(f32[2,1,48,256]{3,2,1,0:T(8,128)S(1)} %get-tuple-element.20), channel_id=1, source_target_pairs={{1,0},{2,1},{3,2},{5,4},{6,5},{7,6}} | collective-permute-start | bytes 294920 | tf_op jit(solution)/shard_map/ppermute | solution.py:23
  100.6 7.5 %collective-permute-start.15 = (f32[2,48,1,256]{3,2,1,0:T(1,128)S(1)}, f32[2,48,1,256]{3,2,1,0:T(1,128)S(1)}, u32[]{:S(2)}, u32[]{:S(2)}) collective-permute-start(f32[2,48,1,256]{3,2,1,0:T(1,128)S(1)} %get-tuple-element.21), channel_id=1, source_target_pairs={{0,4},{1,5},{2,6},{3,7}} | collective-permute-start | bytes 294920 | tf_op jit(solution)/shard_map/ppermute | solution.py:22
  102.1 6.9 %slice-start = ((s8[4718592]{0:T(1024)(128)(4,1)}), s8[4194304]{0:T(1024)(128)(4,1)S(1)}, s32[]{:S(2)}) async-start(s8[4718592]{0:T(1024)(128)(4,1)} %bitcast.41), calls=%async_computation | async-start | bytes 8388608
  102.1 6.9 %slice-start.1 = ((s8[4718592]{0:T(1024)(128)(4,1)}), s8[524288]{0:T(1024)(128)(4,1)S(1)}, s32[]{:S(2)}) async-start(s8[4718592]{0:T(1024)(128)(4,1)} %bitcast.41), calls=%async_computation.1 | async-start | bytes 1048576
  102.1 6.8 %collective-permute-start.14 = (f32[2,48,1,256]{3,2,1,0:T(1,128)S(1)}, f32[2,48,1,256]{3,2,1,0:T(1,128)S(1)}, u32[]{:S(2)}, u32[]{:S(2)}) collective-permute-start(f32[2,48,1,256]{3,2,1,0:T(1,128)S(1)} %get-tuple-element.22), channel_id=1, source_target_pairs={{4,0},{5,1},{6,2},{7,3}} | collective-permute-start | bytes 294920 | tf_op jit(solution)/shard_map/ppermute | solution.py:23
  103.7 6.7 %slice-start.12 = ((s8[4718592]{0:T(1024)(128)(4,1)}), s8[4194304]{0:T(1024)(128)(4,1)S(1)}, s32[]{:S(2)}) async-start(s8[4718592]{0:T(1024)(128)(4,1)} %bitcast.65), calls=%async_computation.12 | async-start | bytes 8388608
  108.1 2.3 slice-start.13
  108.1 2.3 copy-start
  114.4 8.1 %collective-permute-start.16 = (bf16[2,8,48,256]{3,2,1,0:T(8,128)(2,1)S(1)}, bf16[2,8,48,256]{3,2,1,0:T(8,128)(2,1)S(1)}, u32[]{:S(2)}, u32[]{:S(2)}) collective-permute-start(bf16[2,8,48,256]{3,2,1,0:T(8,128)(2,1)S(1)} %get-tuple-element.39), channel_id=1, source_target_pairs={{0,1},{1,2},{2,3},{4,5},{5,6},{6,7}} | collective-permute-start | bytes 1179656 | tf_op jit(solution)/shard_map/ppermute | solution.py:22
  117.8 9.1 %collective-permute-start.17 = (bf16[2,8,48,256]{3,2,1,0:T(8,128)(2,1)S(1)}, bf16[2,8,48,256]{3,2,1,0:T(8,128)(2,1)S(1)}, u32[]{:S(2)}, u32[]{:S(2)}) collective-permute-start(bf16[2,8,48,256]{3,2,1,0:T(8,128)(2,1)S(1)} %get-tuple-element.40), channel_id=1, source_target_pairs={{1,0},{2,1},{3,2},{5,4},{6,5},{7,6}} | collective-permute-start | bytes 1179656 | tf_op jit(solution)/shard_map/ppermute | solution.py:23
  127.0 10.2 %collective-permute-start.18 = (bf16[2,64,8,256]{3,2,1,0:T(8,128)(2,1)S(1)}, bf16[2,64,8,256]{3,2,1,0:T(8,128)(2,1)S(1)}, u32[]{:S(2)}, u32[]{:S(2)}) collective-permute-start(bf16[2,64,8,256]{3,2,1,0:T(8,128)(2,1)S(1)} %get-tuple-element.31), channel_id=1, source_target_pairs={{0,4},{1,5},{2,6},{3,7}} | collective-permute-start | bytes 1572872 | tf_op jit(solution)/shard_map/ppermute | solution.py:22
  130.9 10.5 %collective-permute-start.19 = (bf16[2,64,8,256]{3,2,1,0:T(8,128)(2,1)S(1)}, bf16[2,64,8,256]{3,2,1,0:T(8,128)(2,1)S(1)}, u32[]{:S(2)}, u32[]{:S(2)}) collective-permute-start(bf16[2,64,8,256]{3,2,1,0:T(8,128)(2,1)S(1)} %get-tuple-element.32), channel_id=1, source_target_pairs={{4,0},{5,1},{6,2},{7,3}} | collective-permute-start | bytes 1572872 | tf_op jit(solution)/shard_map/ppermute | solution.py:23
  171.0 8.9 %collective-permute-start.21 = (f32[2,1,48,256]{3,2,1,0:T(8,128)S(1)}, f32[2,1,48,256]{3,2,1,0:T(8,128)S(1)}, u32[]{:S(2)}, u32[]{:S(2)}) collective-permute-start(f32[2,1,48,256]{3,2,1,0:T(8,128)S(1)} %get-tuple-element.15), channel_id=1, source_target_pairs={{0,1},{1,2},{2,3},{4,5},{5,6},{6,7}} | collective-permute-start | bytes 294920 | tf_op jit(solution)/shard_map/ppermute | solution.py:22
  173.2 6.6 %collective-permute-start.20 = (f32[2,1,48,256]{3,2,1,0:T(8,128)S(1)}, f32[2,1,48,256]{3,2,1,0:T(8,128)S(1)}, u32[]{:S(2)}, u32[]{:S(2)}) collective-permute-start(f32[2,1,48,256]{3,2,1,0:T(8,128)S(1)} %get-tuple-element.16), channel_id=1, source_target_pairs={{1,0},{2,1},{3,2},{5,4},{6,5},{7,6}} | collective-permute-start | bytes 294920 | tf_op jit(solution)/shard_map/ppermute | solution.py:23
  176.8 7.6 %collective-permute-start.23 = (f32[2,48,1,256]{3,2,1,0:T(1,128)S(1)}, f32[2,48,1,256]{3,2,1,0:T(1,128)S(1)}, u32[]{:S(2)}, u32[]{:S(2)}) collective-permute-start(f32[2,48,1,256]{3,2,1,0:T(1,128)S(1)} %get-tuple-element.17), channel_id=1, source_target_pairs={{0,4},{1,5},{2,6},{3,7}} | collective-permute-start | bytes 294920 | tf_op jit(solution)/shard_map/ppermute | solution.py:22
  178.3 6.9 %slice-start.2 = ((s8[4718592]{0:T(1024)(128)(4,1)}), s8[4194304]{0:T(1024)(128)(4,1)S(1)}, s32[]{:S(2)}) async-start(s8[4718592]{0:T(1024)(128)(4,1)} %bitcast.48), calls=%async_computation.2 | async-start | bytes 8388608
  178.3 6.9 %slice-start.3 = ((s8[4718592]{0:T(1024)(128)(4,1)}), s8[524288]{0:T(1024)(128)(4,1)S(1)}, s32[]{:S(2)}) async-start(s8[4718592]{0:T(1024)(128)(4,1)} %bitcast.48), calls=%async_computation.3 | async-start | bytes 1048576
  178.3 6.8 %collective-permute-start.22 = (f32[2,48,1,256]{3,2,1,0:T(1,128)S(1)}, f32[2,48,1,256]{3,2,1,0:T(1,128)S(1)}, u32[]{:S(2)}, u32[]{:S(2)}) collective-permute-start(f32[2,48,1,256]{3,2,1,0:T(1,128)S(1)} %get-tuple-element.18), channel_id=1, source_target_pairs={{4,0},{5,1},{6,2},{7,3}} | collective-permute-start | bytes 294920 | tf_op jit(solution)/shard_map/ppermute | solution.py:23
  179.9 6.7 %slice-start.8 = ((s8[4718592]{0:T(1024)(128)(4,1)}), s8[4194304]{0:T(1024)(128)(4,1)S(1)}, s32[]{:S(2)}) async-start(s8[4718592]{0:T(1024)(128)(4,1)} %bitcast.60), calls=%async_computation.8 | async-start | bytes 8388608
  184.4 2.2 slice-start.9
  190.6 8.1 %collective-permute-start.24 = (bf16[2,8,48,256]{3,2,1,0:T(8,128)(2,1)S(1)}, bf16[2,8,48,256]{3,2,1,0:T(8,128)(2,1)S(1)}, u32[]{:S(2)}, u32[]{:S(2)}) collective-permute-start(bf16[2,8,48,256]{3,2,1,0:T(8,128)(2,1)S(1)} %get-tuple-element.37), channel_id=1, source_target_pairs={{0,1},{1,2},{2,3},{4,5},{5,6},{6,7}} | collective-permute-start | bytes 1179656 | tf_op jit(solution)/shard_map/ppermute | solution.py:22
  194.0 9.1 %collective-permute-start.25 = (bf16[2,8,48,256]{3,2,1,0:T(8,128)(2,1)S(1)}, bf16[2,8,48,256]{3,2,1,0:T(8,128)(2,1)S(1)}, u32[]{:S(2)}, u32[]{:S(2)}) collective-permute-start(bf16[2,8,48,256]{3,2,1,0:T(8,128)(2,1)S(1)} %get-tuple-element.38), channel_id=1, source_target_pairs={{1,0},{2,1},{3,2},{5,4},{6,5},{7,6}} | collective-permute-start | bytes 1179656 | tf_op jit(solution)/shard_map/ppermute | solution.py:23
  203.2 10.4 %collective-permute-start.26 = (bf16[2,64,8,256]{3,2,1,0:T(8,128)(2,1)S(1)}, bf16[2,64,8,256]{3,2,1,0:T(8,128)(2,1)S(1)}, u32[]{:S(2)}, u32[]{:S(2)}) collective-permute-start(bf16[2,64,8,256]{3,2,1,0:T(8,128)(2,1)S(1)} %get-tuple-element.29), channel_id=1, source_target_pairs={{0,4},{1,5},{2,6},{3,7}} | collective-permute-start | bytes 1572872 | tf_op jit(solution)/shard_map/ppermute | solution.py:22
  207.2 10.5 %collective-permute-start.27 = (bf16[2,64,8,256]{3,2,1,0:T(8,128)(2,1)S(1)}, bf16[2,64,8,256]{3,2,1,0:T(8,128)(2,1)S(1)}, u32[]{:S(2)}, u32[]{:S(2)}) collective-permute-start(bf16[2,64,8,256]{3,2,1,0:T(8,128)(2,1)S(1)} %get-tuple-element.30), channel_id=1, source_target_pairs={{4,0},{5,1},{6,2},{7,3}} | collective-permute-start | bytes 1572872 | tf_op jit(solution)/shard_map/ppermute | solution.py:23
  247.3 8.9 %collective-permute-start.29 = (f32[2,1,48,256]{3,2,1,0:T(8,128)S(1)}, f32[2,1,48,256]{3,2,1,0:T(8,128)S(1)}, u32[]{:S(2)}, u32[]{:S(2)}) collective-permute-start(f32[2,1,48,256]{3,2,1,0:T(8,128)S(1)} %get-tuple-element.11), channel_id=1, source_target_pairs={{0,1},{1,2},{2,3},{4,5},{5,6},{6,7}} | collective-permute-start | bytes 294920 | tf_op jit(solution)/shard_map/ppermute | solution.py:22
  249.6 6.6 %collective-permute-start.28 = (f32[2,1,48,256]{3,2,1,0:T(8,128)S(1)}, f32[2,1,48,256]{3,2,1,0:T(8,128)S(1)}, u32[]{:S(2)}, u32[]{:S(2)}) collective-permute-start(f32[2,1,48,256]{3,2,1,0:T(8,128)S(1)} %get-tuple-element.12), channel_id=1, source_target_pairs={{1,0},{2,1},{3,2},{5,4},{6,5},{7,6}} | collective-permute-start | bytes 294920 | tf_op jit(solution)/shard_map/ppermute | solution.py:23
  253.2 7.7 %collective-permute-start.31 = (f32[2,48,1,256]{3,2,1,0:T(1,128)S(1)}, f32[2,48,1,256]{3,2,1,0:T(1,128)S(1)}, u32[]{:S(2)}, u32[]{:S(2)}) collective-permute-start(f32[2,48,1,256]{3,2,1,0:T(1,128)S(1)} %get-tuple-element.13), channel_id=1, source_target_pairs={{0,4},{1,5},{2,6},{3,7}} | collective-permute-start | bytes 294920 | tf_op jit(solution)/shard_map/ppermute | solution.py:22
  254.6 6.9 %slice-start.4 = ((s8[4718592]{0:T(1024)(128)(4,1)}), s8[4194304]{0:T(1024)(128)(4,1)S(1)}, s32[]{:S(2)}) async-start(s8[4718592]{0:T(1024)(128)(4,1)} %bitcast.55), calls=%async_computation.4 | async-start | bytes 8388608
  254.6 6.9 %slice-start.5 = ((s8[4718592]{0:T(1024)(128)(4,1)}), s8[524288]{0:T(1024)(128)(4,1)S(1)}, s32[]{:S(2)}) async-start(s8[4718592]{0:T(1024)(128)(4,1)} %bitcast.55), calls=%async_computation.5 | async-start | bytes 1048576
  254.6 6.8 %collective-permute-start.30 = (f32[2,48,1,256]{3,2,1,0:T(1,128)S(1)}, f32[2,48,1,256]{3,2,1,0:T(1,128)S(1)}, u32[]{:S(2)}, u32[]{:S(2)}) collective-permute-start(f32[2,48,1,256]{3,2,1,0:T(1,128)S(1)} %get-tuple-element.14), channel_id=1, source_target_pairs={{4,0},{5,1},{6,2},{7,3}} | collective-permute-start | bytes 294920 | tf_op jit(solution)/shard_map/ppermute | solution.py:23
  256.2 6.7 %slice-start.10 = ((s8[4718592]{0:T(1024)(128)(4,1)}), s8[4194304]{0:T(1024)(128)(4,1)S(1)}, s32[]{:S(2)}) async-start(s8[4718592]{0:T(1024)(128)(4,1)} %bitcast.62), calls=%async_computation.10 | async-start | bytes 8388608
  260.8 2.1 slice-start.11
  265.7 8.1 %collective-permute-start.32 = (bf16[2,8,48,256]{3,2,1,0:T(8,128)(2,1)S(1)}, bf16[2,8,48,256]{3,2,1,0:T(8,128)(2,1)S(1)}, u32[]{:S(2)}, u32[]{:S(2)}) collective-permute-start(bf16[2,8,48,256]{3,2,1,0:T(8,128)(2,1)S(1)} %get-tuple-element.35), channel_id=1, source_target_pairs={{0,1},{1,2},{2,3},{4,5},{5,6},{6,7}} | collective-permute-start | bytes 1179656 | tf_op jit(solution)/shard_map/ppermute | solution.py:22
  269.1 9.1 %collective-permute-start.33 = (bf16[2,8,48,256]{3,2,1,0:T(8,128)(2,1)S(1)}, bf16[2,8,48,256]{3,2,1,0:T(8,128)(2,1)S(1)}, u32[]{:S(2)}, u32[]{:S(2)}) collective-permute-start(bf16[2,8,48,256]{3,2,1,0:T(8,128)(2,1)S(1)} %get-tuple-element.36), channel_id=1, source_target_pairs={{1,0},{2,1},{3,2},{5,4},{6,5},{7,6}} | collective-permute-start | bytes 1179656 | tf_op jit(solution)/shard_map/ppermute | solution.py:23
  278.3 10.5 %collective-permute-start.34 = (bf16[2,64,8,256]{3,2,1,0:T(8,128)(2,1)S(1)}, bf16[2,64,8,256]{3,2,1,0:T(8,128)(2,1)S(1)}, u32[]{:S(2)}, u32[]{:S(2)}) collective-permute-start(bf16[2,64,8,256]{3,2,1,0:T(8,128)(2,1)S(1)} %get-tuple-element.27), channel_id=1, source_target_pairs={{0,4},{1,5},{2,6},{3,7}} | collective-permute-start | bytes 1572872 | tf_op jit(solution)/shard_map/ppermute | solution.py:22
  282.3 10.5 %collective-permute-start.35 = (bf16[2,64,8,256]{3,2,1,0:T(8,128)(2,1)S(1)}, bf16[2,64,8,256]{3,2,1,0:T(8,128)(2,1)S(1)}, u32[]{:S(2)}, u32[]{:S(2)}) collective-permute-start(bf16[2,64,8,256]{3,2,1,0:T(8,128)(2,1)S(1)} %get-tuple-element.28), channel_id=1, source_target_pairs={{4,0},{5,1},{6,2},{7,3}} | collective-permute-start | bytes 1572872 | tf_op jit(solution)/shard_map/ppermute | solution.py:23
where the time goes:
time: 336 us; the launch traced here: 334 us
  starting transfers between devices  85.1 us (25%)
  matrix products  80.8 us (24%)
  waiting for transfers between devices  67.1 us (20%)
  other arithmetic  64.2 us (19%)
  local copies, waits for them, and re-layouts  36.2 us (11%)
    dot_general x4, matrix products, local_sweeps(): jnp.einsum('sqe,sek->sqk', solve_mat, window.reshape(num_sys, ext_size *...  80.8 us
    ppermute x16, starting transfers between devices, grow_halo(): from_below = lax.ppermute(high_edge, axis_name, up_perm(axis_size))  45.8 us
    ppermute x16, waiting for transfers between devices, grow_halo(): from_above = lax.ppermute(low_edge, axis_name, down_perm(axis_size))  36.5 us
    ppermute x16, waiting for transfers between devices, grow_halo(): from_below = lax.ppermute(high_edge, axis_name, up_perm(axis_size))  30.6 us
    ppermute x16, starting transfers between devices, grow_halo(): from_above = lax.ppermute(low_edge, axis_name, down_perm(axis_size))  27.6 us
    dot_general x4, local copies, waits for them, and re-layouts, local_sweeps(): jnp.einsum('sqe,sek->sqk', solve_mat, window.reshape(num_sys, ext_size *...  24.3 us
    mul x4, other arithmetic, apply_local(): flux_x = face_x[..., None] * (wide_x[:, 1:] - wide_x[:, :-1])  18 us
    convert_element_type x4, other arithmetic, local_sweeps(): low_res = residual.astype(jnp.bfloat16)  14.4 us
  transfers between devices with their start and end apart: 36, of which 19 were waited for; matrix products, arithmetic and copies ran while one was open for 9% of the time, Pallas kernels for 0%

commit v1 on v0

v1 whole, which is shorter than its diff:
```python
import jax
import jax.numpy as jnp
from jax import lax
from jax.experimental import pallas as pl
from jax.experimental.pallas import tpu as pltpu
from jax.sharding import PartitionSpec as P

SWEEPS = 4
SUB = 48
MARGIN = 8
EXT = 64
SYS = 2
RHS = 256
STRIPS = 3
WIDE = 16
LANES = 128
F32 = jnp.float32
BF16 = jnp.bfloat16


def both(face):
    return jnp.concatenate([face, face], axis=1)


def roll_down(values):
    return pltpu.roll(values, 1, 0)


def roll_up(values):
    return pltpu.roll(values, values.shape[0] - 1, 0)


def kernel(f_hbm, u0_hbm, c_ref, s_hbm, om_ref, out_hbm,
           mat, res, apx, cor, win, fx, fy, fyr,
           wys, wxs, wyr, wxr, wcr, zys, zyr, cxr, cyr,
           mat_sem, u_sem, f_sem, out_sem,
           wy_ss, wy_rs, wx_ss, wx_rs, wc_ss, wc_rs,
           zy_ss, zy_rs, zx_ss, zx_rs, cx_ss, cx_rs, cy_ss, cy_rs):
    row = lax.axis_index("row")
    col = lax.axis_index("col")
    has_up = row > 0
    has_dn = row < 3
    left_side = col == 0
    strip_a = 2 * (1 - col)
    strip_c = 2 * col
    tile_off = pl.multiple_of(8 * (1 - col), 8)
    tile_oth = pl.multiple_of(8 * col, 8)
    has_nb = (has_up, has_dn)
    steps = (-1, 1)

    def remote(src, dst, ss, rs, drow, dcol):
        return pltpu.make_async_remote_copy(
            src_ref=src, dst_ref=dst, send_sem=ss, recv_sem=rs,
            device_id={"row": row + drow, "col": col + dcol * (1 - 2 * col)},
            device_id_type=pl.DeviceIdType.MESH)

    def zy_copy(s, par):
        return remote(zys.at[s], zyr.at[par, s], zy_ss.at[s], zy_rs.at[par, s], 0, 1)

    def zx_copy(src, s, d, q):
        start, land = ((1, SUB + 1), (SUB, 0))[d]
        return remote(src.at[s, q, start], src.at[s, q, land], zx_ss.at[s, d, q], zx_rs.at[s, d, q], steps[d], 0)

    def wy_copy(s):
        return remote(wys.at[s], wyr.at[s], wy_ss.at[s], wy_rs.at[s], 0, 1)

    def wx_copy(s, d):
        return remote(wxs.at[s, d], wxr.at[s, d], wx_ss.at[s, d], wx_rs.at[s, d], steps[d], 0)

    def wc_copy(s, d, par):
        first = (0, SUB - MARGIN)[d]
        return remote(wys.at[s, pl.ds(first, MARGIN)], wcr.at[par, s, d], wc_ss.at[par, s, d], wc_rs.at[par, s, d], steps[d], 1)

    def cx_copy(d):
        first = (0, SUB - 8)[d]
        return remote(c_ref.at[:, pl.ds(first, 8), :], cxr.at[d], cx_ss.at[d], cx_rs.at[d], steps[d], 0)

    def cy_copy():
        return remote(c_ref, cyr, cy_ss, cy_rs, 0, 1)

    def start_x(make):
        for d in range(2):
            @pl.when(has_nb[d])
            def _():
                make(d).start()

    def wait_x(make):
        for d in range(2):
            @pl.when(has_nb[d])
            def _():
                make(d).wait_send()

            @pl.when(has_nb[1 - d])
            def _():
                make(d).wait_recv()

    for s in range(SYS):
        for q in range(STRIPS):
            for halo in (0, SUB + 1):
                apx[s, q, halo] = jnp.zeros((WIDE, RHS), F32)
                cor[s, q, halo] = jnp.zeros((WIDE, RHS), F32)

    barrier = pltpu.get_barrier_semaphore()
    for drow in (-1, 0, 1):
        for dcol in (0, 1):
            if drow == 0 and dcol == 0:
                continue

            def greet():
                pl.semaphore_signal(barrier, inc=1, device_id={"row": row + drow, "col": col + dcol * (1 - 2 * col)},
                                    device_id_type=pl.DeviceIdType.MESH)
            if drow == 0:
                greet()
            else:
                pl.when(has_nb[(drow + 1) // 2])(greet)

    def u_load(s, q):
        return pltpu.make_async_copy(u0_hbm.at[s, :, q], apx.at[s, q, pl.ds(1, SUB)], u_sem.at[s, q])

    def f_load(s, q):
        return pltpu.make_async_copy(f_hbm.at[s, :, q], res.at[s, q], f_sem.at[s, q])

    def mat_load(s, q):
        return pltpu.make_async_copy(s_hbm.at[s, :, q], mat.at[s, q], mat_sem.at[s, q])

    for s in range(SYS):
        for q in range(STRIPS):
            u_load(s, q).start()
        for q in range(STRIPS):
            f_load(s, q).start()
    for s in range(SYS):
        for q in (strip_a, 1, strip_c):
            mat_load(s, q).start()

    @pl.loop(0, SYS * EXT * EXT // 256)
    def _(t):
        rows = pl.ds(pl.multiple_of(t * 256, 256), 256)
        win[rows, :] = jnp.zeros((256, RHS), BF16)

    @pl.when(jnp.logical_not(has_up))
    def _():
        for s in range(SYS):
            cxr[1, s, 7:8, :] = c_ref[s, 0:1, :]

    @pl.when(jnp.logical_not(has_dn))
    def _():
        for s in range(SYS):
            cxr[0, s, 0:1, :] = c_ref[s, SUB - 1:SUB, :]

    pl.semaphore_wait(barrier, 1 + 2 * has_up.astype(jnp.int32) + 2 * has_dn.astype(jnp.int32))
    cy_copy().start()
    start_x(cx_copy)

    def send_zy(src, s, par):
        @pl.loop(0, SUB)
        def _(i):
            tile = src[s, strip_a, i + 1, pl.ds(tile_off, 8), :]
            zys[s, i] = jnp.where(left_side, tile[7:8], tile[0:1])
        zy_copy(s, par).start()

    def send_zx(src, s, q):
        start_x(lambda d: zx_copy(src, s, d, q))

    for s in range(SYS):
        for q in range(STRIPS):
            u_load(s, q).wait()
        send_zy(apx, s, 0)
        for q in range(STRIPS):
            send_zx(apx, s, q)

    cy_copy().wait()
    wait_x(cx_copy)
    eye = (lax.broadcasted_iota(jnp.int32, (SUB, SUB), 0) == lax.broadcasted_iota(jnp.int32, (SUB, SUB), 1)).astype(F32)
    lane = lax.broadcasted_iota(jnp.int32, (1, SUB), 1)
    near = (lane == jnp.where(left_side, 0, SUB - 1)).astype(F32)

    def spread(line):
        cells = jnp.sum(jnp.broadcast_to(line, (SUB, SUB)) * eye, axis=1, keepdims=True)
        return jnp.broadcast_to(cells, (SUB, LANES))

    for s in range(SYS):
        def one_row(i, before, s=s):
            line = c_ref[s, pl.ds(i, 1), :]
            here = spread(line)
            face = 0.5 * (before + here)
            other = jnp.broadcast_to(jnp.sum(cyr[s, pl.ds(i, 1), :] * near, axis=1, keepdims=True), (8, LANES))
            first = jnp.broadcast_to(here[0:1], (8, LANES))
            last = jnp.broadcast_to(here[SUB - 1:SUB], (8, LANES))
            beyond = jnp.where(left_side, first, other)
            low = 0.5 * (roll_down(jnp.concatenate([here, beyond], axis=0))[0:SUB] + here)
            high = 0.5 * (last + jnp.where(left_side, other, last))
            for q in range(STRIPS):
                fx[s, q, i] = face[q * WIDE:(q + 1) * WIDE]
                fy[s, q, i] = low[q * WIDE:(q + 1) * WIDE]
            fyr[s, i] = high[0:1]
            return here
        last_row = lax.fori_loop(0, SUB, one_row, spread(cxr[1, s, 7:8, :]))
        face = 0.5 * (last_row + spread(cxr[0, s, 0:1, :]))
        for q in range(STRIPS):
            fx[s, q, SUB] = face[q * WIDE:(q + 1) * WIDE]

    sub = lax.broadcasted_iota(jnp.int32, (8, RHS), 0)
    sub_face = lax.broadcasted_iota(jnp.int32, (8, LANES), 0)

    def frame(src, s, par, scale):
        @pl.loop(0, SUB)
        def _(i):
            near_cols, far_cols = pl.ds(tile_off, 8), pl.ds(tile_oth, 8)
            here = src[s, strip_a, i + 1, near_cols, :]
            inner = src[s, strip_a, i + 1, far_cols, :]
            edge = jnp.broadcast_to(zyr[par, s, i], (8, RHS))
            before = jnp.where(left_side, inner, edge)
            after = jnp.where(left_side, edge, inner)
            lower = jnp.where(sub == 0, roll_down(before), roll_down(here))
            upper = jnp.where(sub == 7, roll_up(after), roll_up(here))
            face = fy[s, strip_a, i, near_cols, :]
            face_after = jnp.where(left_side, jnp.broadcast_to(fyr[s, i], (8, LANES)), fy[s, strip_a, i, far_cols, :])
            face_up = jnp.where(sub_face == 7, roll_up(face_after), roll_up(face))
            applied = both(fx[s, strip_a, i, near_cols, :]) * (here - src[s, strip_a, i, near_cols, :])
            applied += both(fx[s, strip_a, i + 1, near_cols, :]) * (here - src[s, strip_a, i + 2, near_cols, :])
            applied += both(face) * (here - lower)
            applied += both(face_up) * (here - upper)
            wys[s, i] = (res[s, strip_a, i, near_cols, :] - scale * applied).astype(BF16)

    def send_frame(s, par):
        wy_copy(s).start()
        start_x(lambda d: wc_copy(s, d, par))

    def finish(src, s, par, scale, update):
        gap = jnp.zeros((MARGIN, RHS), F32)
        base = s * (EXT * EXT)

        def strips(ref, i):
            return jnp.concatenate([ref[s, q, i] for q in range(STRIPS)], axis=0)

        @pl.loop(0, SUB)
        def _(i):
            here = strips(src, i + 1)
            edge = jnp.broadcast_to(zyr[par, s, i], (8, RHS))
            none = jnp.zeros_like(edge)
            lower = roll_down(jnp.concatenate([here, jnp.where(left_side, none, edge)], axis=0))[0:SUB]
            upper = roll_up(jnp.concatenate([here, jnp.where(left_side, edge, none)], axis=0))[0:SUB]
            face = strips(fy, i)
            face_up = roll_up(jnp.concatenate([face, jnp.broadcast_to(fyr[s, i], (8, LANES))], axis=0))[0:SUB]
            applied = both(strips(fx, i)) * (here - strips(src, i))
            applied += both(strips(fx, i + 1)) * (here - strips(src, i + 2))
            applied += both(face) * (here - lower)
            applied += both(face_up) * (here - upper)
            new = strips(res, i) - scale * applied
            for q in range(STRIPS):
                res[s, q, i] = new[q * WIDE:(q + 1) * WIDE]
            if update:
                for q in range(STRIPS):
                    apx[s, q, i + 1] += scale * src[s, q, i + 1]
            rows = pl.ds(pl.multiple_of(base + (i + MARGIN) * EXT, EXT), EXT)
            win[rows, :] = jnp.concatenate([gap, new, gap], axis=0).astype(BF16)

        @pl.loop(0, MARGIN)
        def _(e):
            wxs[s, 0, e] = strips(res, e).astype(BF16)
            wxs[s, 1, e] = strips(res, e + SUB - MARGIN).astype(BF16)
        start_x(lambda d: wx_copy(s, d))

    def wait_edges(src, s):
        zy_copy(s, 0).wait()
        for q in range(STRIPS):
            wait_x(lambda d: zx_copy(src, s, d, q))

    def fill_halo(s, par):
        base = s * (EXT * EXT)
        wy_copy(s).wait()
        start = pl.multiple_of(SUB * (1 - col), WIDE)

        @pl.loop(0, SUB)
        def _(i):
            rows = pl.ds(pl.multiple_of(base + (i + MARGIN) * EXT + start, WIDE), WIDE)
            old = win[rows, :].astype(F32)
            new = wyr[s, i].astype(F32)
            on_right = jnp.concatenate([old[0:8], new], axis=0)
            on_left = jnp.concatenate([new, old[8:16]], axis=0)
            win[rows, :] = jnp.where(left_side, on_right, on_left).astype(BF16)

        wait_x(lambda d: wx_copy(s, d))
        wait_x(lambda d: wc_copy(s, d, par))
        gap = jnp.zeros((MARGIN, RHS), F32)
        for d in range(2):
            first = (MARGIN + SUB, 0)[d]

            @pl.when(has_nb[1 - d])
            def _():
                @pl.loop(0, MARGIN)
                def _(e):
                    rows = pl.ds(pl.multiple_of(base + (first + e) * EXT, EXT), EXT)
                    corner = wcr[par, s, d, e].astype(F32)
                    parts = [jnp.where(left_side, gap, corner), wxr[s, d, e].astype(F32), jnp.where(left_side, corner, gap)]
                    win[rows, :] = jnp.concatenate(parts, axis=0).astype(BF16)

    def multiply(s, q, first, count):
        window = win[pl.ds(pl.multiple_of(s * (EXT * EXT), EXT * EXT), EXT * EXT), :]
        rows = mat[s, q, first:first + count].reshape(count * WIDE, EXT * EXT)
        out = jnp.dot(rows, window, preferred_element_type=F32)
        cor[s, q, 1 + first:1 + first + count] = out.reshape(count, WIDE, RHS)

    for s in range(SYS):
        for q in range(STRIPS):
            f_load(s, q).wait()
        wait_edges(apx, s)
        frame(apx, s, 0, 1.0)
        send_frame(s, 0)
        finish(apx, s, 0, 1.0, False)

    def out_store(s, q):
        return pltpu.make_async_copy(apx.at[s, q, pl.ds(1, SUB)], out_hbm.at[s, :, q], out_sem.at[s, q])

    def half_sweep(h, carry):
        k = h // 2
        s = h % 2
        par = k % 2
        more = k < SWEEPS - 1
        first_time = k == 0
        scale = om_ref[s]

        def last_strip(q):
            @pl.when(jnp.logical_not(more))
            def _():
                @pl.loop(0, SUB)
                def _(i):
                    apx[s, q, i + 1] += scale * cor[s, q, i + 1]
                out_store(s, q).start()

        def wait_mat(q):
            @pl.when(first_time)
            def _():
                mat_load(s, q).wait()

        fill_halo(s, par)
        wait_mat(strip_a)
        multiply(s, strip_a, 0, SUB)

        @pl.when(more)
        def _():
            send_zy(cor, s, 1 - par)
            send_zx(cor, s, strip_a)
        last_strip(strip_a)

        @pl.when(jnp.logical_and(h > 0, h < 2 * SWEEPS - 1))
        def _():
            s_old = 1 - s
            for q in (1, strip_c):
                wait_x(lambda d: zx_copy(cor, s_old, d, q))
            finish(cor, s_old, ((h - 1) // 2 + 1) % 2, om_ref[s_old], True)

        wait_mat(1)
        multiply(s, 1, 0, SUB)

        @pl.when(more)
        def _():
            send_zx(cor, s, 1)
        last_strip(1)

        wait_mat(strip_c)
        multiply(s, strip_c, 0, SUB // 2)

        @pl.when(more)
        def _():
            zy_copy(s, 1 - par).wait()
            wait_x(lambda d: zx_copy(cor, s, d, strip_a))
            frame(cor, s, 1 - par, scale)
            send_frame(s, 1 - par)

        multiply(s, strip_c, SUB // 2, SUB // 2)

        @pl.when(more)
        def _():
            send_zx(cor, s, strip_c)
        last_strip(strip_c)
        return carry

    lax.fori_loop(0, 2 * SWEEPS, half_sweep, 0)
    for s in range(SYS):
        for q in range(STRIPS):
            out_store(s, q).wait()


def local_solve(forcing, init_guess, cell_coef, solve_rows, relax_factor):
    forcing = forcing.reshape(SYS, SUB, STRIPS, WIDE, RHS)
    init_guess = init_guess.reshape(SYS, SUB, STRIPS, WIDE, RHS)
    mats = solve_rows.reshape(SYS, SUB, STRIPS, WIDE, EXT * EXT)
    hbm = pl.BlockSpec(memory_space=pl.ANY)
    dma = pltpu.SemaphoreType.DMA
    out = pl.pallas_call(
        kernel,
        out_shape=jax.ShapeDtypeStruct((SYS, SUB, STRIPS, WIDE, RHS), F32),
        in_specs=[hbm, hbm, pl.BlockSpec(memory_space=pltpu.VMEM), hbm, pl.BlockSpec(memory_space=pltpu.SMEM)],
        out_specs=hbm,
        scratch_shapes=[
            pltpu.VMEM((SYS, STRIPS, SUB, WIDE, EXT * EXT), BF16),
            pltpu.VMEM((SYS, STRIPS, SUB, WIDE, RHS), F32),
            pltpu.VMEM((SYS, STRIPS, SUB + 2, WIDE, RHS), F32),
            pltpu.VMEM((SYS, STRIPS, SUB + 2, WIDE, RHS), F32),
            pltpu.VMEM((SYS * EXT * EXT, RHS), BF16),
            pltpu.VMEM((SYS, STRIPS, SUB + 1, WIDE, LANES), F32),
            pltpu.VMEM((SYS, STRIPS, SUB, WIDE, LANES), F32),
            pltpu.VMEM((SYS, SUB, 1, LANES), F32),
            pltpu.VMEM((SYS, SUB, MARGIN, RHS), BF16),
            pltpu.VMEM((SYS, 2, MARGIN, SUB, RHS), BF16),
            pltpu.VMEM((SYS, SUB, MARGIN, RHS), BF16),
            pltpu.VMEM((SYS, 2, MARGIN, SUB, RHS), BF16),
            pltpu.VMEM((2, SYS, 2, MARGIN, MARGIN, RHS), BF16),
            pltpu.VMEM((SYS, SUB, 1, RHS), F32),
            pltpu.VMEM((2, SYS, SUB, 1, RHS), F32),
            pltpu.VMEM((2, SYS, 8, SUB), F32),
            pltpu.VMEM((SYS, SUB, SUB), F32),
            dma((SYS, STRIPS)), dma((SYS, STRIPS)), dma((SYS, STRIPS)), dma((SYS, STRIPS)),
            dma((SYS,)), dma((SYS,)), dma((SYS, 2)), dma((SYS, 2)), dma((2, SYS, 2)), dma((2, SYS, 2)),
            dma((SYS,)), dma((2, SYS)), dma((SYS, 2, STRIPS)), dma((SYS, 2, STRIPS)),
            dma((2,)), dma((2,)), dma(()), dma(()),
        ],
        compiler_params=pltpu.CompilerParams(
            collective_id=0, has_side_effects=True, vmem_limit_bytes=67_043_328),
    )(forcing, init_guess, cell_coef, mats, relax_factor)
    return out.reshape(SYS, SUB, SUB, RHS)


def solution(mesh):
    grid_spec = P(None, "row", "col", None)
    return jax.shard_map(
        local_solve, mesh=mesh,
        in_specs=(grid_spec, grid_spec, P(None, "row", "col"), P(None, "row", "col", None, None), P(None)),
        out_specs=grid_spec, check_vma=False)
```

time: 336 us -> 151 us (0.45)
  Pallas kernels: 0 us -> 146 us
  starting transfers between devices: 85.1 us -> 0 us
  matrix products: 80.8 us -> 0 us
  waiting for transfers between devices: 67.1 us -> 0 us
  other arithmetic: 64.2 us -> 0 us
  local copies, waits for them, and re-layouts: 36.2 us -> 4.86 us
    pallas_call x0 -> x1, Pallas kernels: none -> 146 us  [local_solve(): pl.pallas_call(kernel, out_shape=jax.ShapeDtypeStruct((SYS, SUB, STRIPS,...]
    ppermute x36 -> x0, starting transfers between devices: 85.1 us -> none  [the longest x16 45.8 us: grow_halo(): from_below = lax.ppermute(high_edge, axis_name, up_perm(axis_size))]
    dot_general x4 -> x0, matrix products: 80.8 us -> none  [local_sweeps(): jnp.einsum('sqe,sek->sqk', solve_mat, window.reshape(num_sys, ext_size *...]
    ppermute x36 -> x0, waiting for transfers between devices: 67.1 us -> none  [the longest x16 36.5 us: grow_halo(): from_above = lax.ppermute(low_edge, axis_name, down_perm(axis_size))]
    mul x10 -> x0, other arithmetic: 25.7 us -> none  [the longest x4 18 us: apply_local(): flux_x = face_x[..., None] * (wide_x[:, 1:] - wide_x[:, :-1])]
    dot_general x4 -> x0, local copies, waits for them, and re-layouts: 24.3 us -> none  [local_sweeps(): jnp.einsum('sqe,sek->sqk', solve_mat, window.reshape(num_sys, ext_size *...]
    convert_element_type x4 -> x0, other arithmetic: 14.4 us -> none  [local_sweeps(): low_res = residual.astype(jnp.bfloat16)]
    add x1 -> x0, other arithmetic: 12.9 us -> none  [local_sweeps(): approx = approx + step_size * correction]
  transfers between devices with their start and end apart: 36 -> 0, of which waited for: 19 -> 0; matrix products, arithmetic and copies ran while one was open for 9% -> 0% of each run, Pallas kernels for 0% -> 0%
where the time goes in v1:
time: 151 us
  Pallas kernels  146 us (97%)
  local copies, waits for them, and re-layouts  4.86 us (3%)
    pallas_call x1, Pallas kernels, local_solve(): pl.pallas_call(kernel, out_shape=jax.ShapeDtypeStruct((SYS, SUB, STRIPS,...  146 us
    unnamed x1, local copies, waits for them, and re-layouts  4.86 us

profile of v1, /device:TPU:1, one launch (start us, length us, event | category | flops | bytes accessed | tf_op | source)
XLA Modules:
  0.0 150.9 jit_solution(10319279091394029312)
XLA Ops:
  0.0 146.1 %shard_map.55 = f32[2,48,3,16,256]{4,3,2,1,0:T(8,128)} custom-call(f32[2,48,3,16,256]{4,3,2,1,0:T(8,128)} %bitcast.6, f32[2,48,3,16,256]{4,3,2,1,0:T(8,128)} %bitcast.7, f32[2,48,48]{2,1,0:T(8,128)} %c_ref.1, bf16[2,48,3,16,4096]{4,3,2,1,0:T(8,128)(2,1)} %bitcast.4, f32[2]{0:T(128)} %om_ref.1), custom_call_target="tpu_custom_call" | custom-call | tf_op jit(solution)/shard_map/pallas_call | solution.py:391
  146.1 4.9 %copy.7 = f32[2,48,48,256]{3,2,1,0:T(8,128)} copy(f32[2,48,48,256]{3,2,1,0:T(8,128)} %bitcast.5) | data formatting | bytes 9437184

commit v2 on v1

v2 whole, which is shorter than its diff:
```python
import jax
import jax.numpy as jnp
from jax import lax
from jax.experimental import pallas as pl
from jax.experimental.pallas import tpu as pltpu
from jax.sharding import PartitionSpec as P

SWEEPS = 4
SUB = 48
MARGIN = 8
EXT = 64
SYS = 2
RHS = 256
STRIPS = 3
WIDE = 16
LANES = 128
PIECE = 12
TILES = 16
F32 = jnp.float32
BF16 = jnp.bfloat16


def both(face):
    return jnp.concatenate([face, face], axis=1)


def roll_down(values):
    return pltpu.roll(values, 1, 0)


def roll_up(values):
    return pltpu.roll(values, values.shape[0] - 1, 0)


def kernel(f_hbm, u0_hbm, c_ref, s_hbm, om_ref, out_hbm,
           mat, res, apx, cor0, cor1, win0, win1, fx, fy, fyr,
           wys, wxs, wyr, wxr, wcr, zys, zyr, cxr, cyr,
           mat_sem, u_sem, f_sem, out_sem,
           wy_ss, wy_rs, wx_ss, wx_rs, wc_ss, wc_rs,
           zy_ss, zy_rs, zx_ss, zx_rs, cx_ss, cx_rs, cy_ss, cy_rs):
    row = lax.axis_index("row")
    col = lax.axis_index("col")
    has_up = row > 0
    has_dn = row < 3
    left_side = col == 0
    strip_a = 2 * (1 - col)
    strip_c = 2 * col
    tile_off = pl.multiple_of(8 * (1 - col), 8)
    tile_oth = pl.multiple_of(8 * col, 8)
    has_nb = (has_up, has_dn)
    cors, wins = (cor0, cor1), (win0, win1)
    steps = (-1, 1)

    def remote(src, dst, ss, rs, drow, dcol):
        return pltpu.make_async_remote_copy(
            src_ref=src, dst_ref=dst, send_sem=ss, recv_sem=rs,
            device_id={"row": row + drow, "col": col + dcol * (1 - 2 * col)},
            device_id_type=pl.DeviceIdType.MESH)

    def zy_copy(s, par):
        return remote(zys.at[s], zyr.at[par, s], zy_ss.at[s], zy_rs.at[par, s], 0, 1)

    def zx_copy(s, d, q):
        start, land = ((1, SUB + 1), (SUB, 0))[d]
        return remote(cors[s].at[q, start], cors[s].at[q, land], zx_ss.at[s, d, q], zx_rs.at[s, d, q], steps[d], 0)

    def wy_copy(s, part):
        rows = pl.ds(*((0, MARGIN), (SUB - MARGIN, MARGIN), (MARGIN, SUB - 2 * MARGIN))[part])
        return remote(wys.at[s, rows], wyr.at[s, rows], wy_ss.at[s, part], wy_rs.at[s, part], 0, 1)

    def wx_copy(s, d):
        return remote(wxs.at[s, d], wxr.at[s, d], wx_ss.at[s, d], wx_rs.at[s, d], steps[d], 0)

    def wc_copy(s, d, par):
        first = (0, SUB - MARGIN)[d]
        return remote(wyr.at[s, pl.ds(first, MARGIN)], wcr.at[par, s, d], wc_ss.at[par, s, d], wc_rs.at[par, s, d], steps[d], 0)

    def cx_copy(d):
        first = (0, SUB - 8)[d]
        return remote(c_ref.at[:, pl.ds(first, 8), :], cxr.at[d], cx_ss.at[d], cx_rs.at[d], steps[d], 0)

    def cy_copy():
        return remote(c_ref, cyr, cy_ss, cy_rs, 0, 1)

    def start_x(make):
        for d in range(2):
            @pl.when(has_nb[d])
            def _():
                make(d).start()

    def wait_x(make):
        for d in range(2):
            @pl.when(has_nb[d])
            def _():
                make(d).wait_send()

            @pl.when(has_nb[1 - d])
            def _():
                make(d).wait_recv()

    for s in range(SYS):
        for q in range(STRIPS):
            for halo in (0, SUB + 1):
                cors[s][q, halo] = jnp.zeros((WIDE, RHS), F32)

    barrier = pltpu.get_barrier_semaphore()
    def greet(drow, dcol):
        pl.semaphore_signal(barrier, inc=1, device_id={"row": row + drow, "col": col + dcol * (1 - 2 * col)},
                            device_id_type=pl.DeviceIdType.MESH)

    greet(0, 1)
    for d in range(2):
        @pl.when(has_nb[d])
        def _():
            greet(steps[d], 0)

    def u_load(s, q):
        return pltpu.make_async_copy(u0_hbm.at[s, :, q], cors[s].at[q, pl.ds(1, SUB)], u_sem.at[s, q])

    def f_load(s, q):
        return pltpu.make_async_copy(f_hbm.at[s, :, q], res.at[s, q], f_sem.at[s, q])

    def apx_load(s, q):
        return pltpu.make_async_copy(u0_hbm.at[s, :, q], apx.at[s, q], out_sem.at[s, q])

    def mat_load(s, q, t):
        return pltpu.make_async_copy(s_hbm.at[s, :, q, :, pl.ds(256 * t, 256)], mat.at[s, q, t], mat_sem.at[s, q, t])

    order = (strip_a, 1, strip_c)
    for load in (u_load, f_load):
        for s in range(SYS):
            for q in range(STRIPS):
                load(s, q).start()
    for q in order:
        for t in range(TILES):
            mat_load(0, q, t).start()
    for s in (1, 0):
        for q in range(STRIPS):
            apx_load(s, q).start()
    for q in order:
        for t in range(TILES):
            mat_load(1, q, t).start()

    for s in range(SYS):
        @pl.loop(0, EXT * EXT // 256)
        def _(t):
            rows = pl.ds(pl.multiple_of(t * 256, 256), 256)
            wins[s][rows, :] = jnp.zeros((256, RHS), BF16)

    for d, line, edge in ((1, 7, 0), (0, 0, SUB - 1)):
        @pl.when(jnp.logical_not(has_nb[1 - d]))
        def _():
            for s in range(SYS):
                cxr[d, s, line:line + 1, :] = c_ref[s, edge:edge + 1, :]
                for e in range(MARGIN):
                    wxr[s, d, e] = jnp.zeros((SUB, RHS), BF16)
                    for par in range(2):
                        wcr[par, s, d, e] = jnp.zeros((MARGIN, RHS), BF16)

    pl.semaphore_wait(barrier, 1 + has_up.astype(jnp.int32) + has_dn.astype(jnp.int32))
    cy_copy().start()
    start_x(cx_copy)

    def send_zy(s, par):
        @pl.loop(0, SUB, unroll=8)
        def _(i):
            tile = cors[s][strip_a, i + 1, pl.ds(tile_off, 8), :]
            zys[s, i] = jnp.where(left_side, tile[7:8], tile[0:1])
        zy_copy(s, par).start()

    def send_zx(s, q):
        start_x(lambda d: zx_copy(s, d, q))

    for s in range(SYS):
        for q in range(STRIPS):
            u_load(s, q).wait()
        send_zy(s, 0)
        for q in range(STRIPS):
            send_zx(s, q)

    cy_copy().wait()
    wait_x(cx_copy)
    eye = (lax.broadcasted_iota(jnp.int32, (SUB, SUB), 0) == lax.broadcasted_iota(jnp.int32, (SUB, SUB), 1)).astype(F32)
    lane = lax.broadcasted_iota(jnp.int32, (1, SUB), 1)
    near = (lane == jnp.where(left_side, 0, SUB - 1)).astype(F32)

    def spread(line):
        cells = jnp.sum(jnp.broadcast_to(line, (SUB, SUB)) * eye, axis=1, keepdims=True)
        return jnp.broadcast_to(cells, (SUB, LANES))

    def coefficients(s):
        def one_row(i, before):
            line = c_ref[s, pl.ds(i, 1), :]
            here = spread(line)
            face = 0.5 * (before + here)
            other = jnp.broadcast_to(jnp.sum(cyr[s, pl.ds(i, 1), :] * near, axis=1, keepdims=True), (8, LANES))
            first = jnp.broadcast_to(here[0:1], (8, LANES))
            last = jnp.broadcast_to(here[SUB - 1:SUB], (8, LANES))
            beyond = jnp.where(left_side, first, other)
            low = 0.5 * (roll_down(jnp.concatenate([here, beyond], axis=0))[0:SUB] + here)
            high = 0.5 * (last + jnp.where(left_side, other, last))
            for q in range(STRIPS):
                fx[s, q, i] = face[q * WIDE:(q + 1) * WIDE]
                fy[s, q, i] = low[q * WIDE:(q + 1) * WIDE]
            fyr[s, i] = high[0:1]
            return here
        last_row = lax.fori_loop(0, SUB, one_row, spread(cxr[1, s, 7:8, :]), unroll=4)
        face = 0.5 * (last_row + spread(cxr[0, s, 0:1, :]))
        for q in range(STRIPS):
            fx[s, q, SUB] = face[q * WIDE:(q + 1) * WIDE]

    sub = lax.broadcasted_iota(jnp.int32, (8, RHS), 0)
    sub_face = lax.broadcasted_iota(jnp.int32, (8, LANES), 0)

    def frame_row(s, par, scale, i):
        near_cols, far_cols = pl.ds(tile_off, 8), pl.ds(tile_oth, 8)
        here = cors[s][strip_a, i + 1, near_cols, :]
        inner = cors[s][strip_a, i + 1, far_cols, :]
        edge = jnp.broadcast_to(zyr[par, s, i], (8, RHS))
        before = jnp.where(left_side, inner, edge)
        after = jnp.where(left_side, edge, inner)
        lower = jnp.where(sub == 0, roll_down(before), roll_down(here))
        upper = jnp.where(sub == 7, roll_up(after), roll_up(here))
        face = fy[s, strip_a, i, near_cols, :]
        face_after = jnp.where(left_side, jnp.broadcast_to(fyr[s, i], (8, LANES)), fy[s, strip_a, i, far_cols, :])
        face_up = jnp.where(sub_face == 7, roll_up(face_after), roll_up(face))
        applied = both(fx[s, strip_a, i, near_cols, :]) * (here - cors[s][strip_a, i, near_cols, :])
        applied += both(fx[s, strip_a, i + 1, near_cols, :]) * (here - cors[s][strip_a, i + 2, near_cols, :])
        applied += both(face) * (here - lower)
        applied += both(face_up) * (here - upper)
        wys[s, i] = (res[s, strip_a, i, near_cols, :] - scale * applied).astype(BF16)

    def frame(s, par, scale):
        @pl.loop(0, SUB, unroll=8)
        def _(i):
            frame_row(s, par, scale, i)

    def send_frame(s):
        for part in range(3):
            wy_copy(s, part).start()

    def send_corners(s, par):
        for part in range(2):
            wy_copy(s, part).wait()
        start_x(lambda d: wc_copy(s, d, par))

    def strips(ref, i):
        return jnp.concatenate([ref[q, i] for q in range(STRIPS)], axis=0)

    def finish_row(s, par, scale, gain, i, frame_row=None, below=None):
        gap = jnp.zeros((MARGIN, RHS), F32)
        src = cors[s]
        here = strips(src, i + 1)
        edge = jnp.broadcast_to(zyr[par, s, i], (8, RHS))
        none = jnp.zeros_like(edge)
        before = roll_down(jnp.concatenate([here, jnp.where(left_side, none, edge)], axis=0))
        wide = jnp.concatenate([here, jnp.where(left_side, edge, none)], axis=0)
        face = jnp.concatenate([strips(fy.at[s], i), jnp.broadcast_to(fyr[s, i], (8, LANES))], axis=0)
        flux = both(face) * (wide - before)
        if below is None:
            below = both(strips(fx.at[s], i)) * (here - strips(src, i))
        above = both(strips(fx.at[s], i + 1)) * (strips(src, i + 2) - here)
        applied = (below - above) + (flux[0:SUB] - roll_up(flux)[0:SUB])
        new = strips(res.at[s], i) - scale * applied
        for q in range(STRIPS):
            res[s, q, i] = new[q * WIDE:(q + 1) * WIDE]
            if gain is not None:
                apx[s, q, i] += gain * here[q * WIDE:(q + 1) * WIDE]
        start = (i + MARGIN) * EXT
        rows = pl.ds(start if isinstance(i, int) else pl.multiple_of(start, EXT), EXT)
        wins[s][rows, :] = jnp.concatenate([gap, new, gap], axis=0).astype(BF16)
        if frame_row is not None:
            wxs[(s,) + frame_row] = new.astype(BF16)
        return above

    def finish_rows(s, par, scale, gain, rows, ends):
        held = [None]

        def one(i, first, frame_row):
            held[0] = finish_row(s, par, scale, gain, i, frame_row, None if first else held[0])
        works = []
        for n, i in enumerate(rows):
            frame_row = None if not ends else ((0, i) if i < MARGIN else (1, i - SUB + MARGIN))
            works.append(lambda i=i, first=(n == 0 or rows[n - 1] != i - 1), f=frame_row: one(i, first, f))
        return works

    END_ROWS = list(range(MARGIN)) + list(range(SUB - MARGIN, SUB))

    def send_ends(s):
        start_x(lambda d: wx_copy(s, d))

    def wait_edges(s, which):
        for q in which:
            wait_x(lambda d: zx_copy(s, d, q))

    def fill_tile(s, par, t):
        gap = jnp.zeros((MARGIN, RHS), F32)
        for e in range(4 * t, 4 * t + 4):
            i = e - MARGIN
            if 0 <= i < SUB:
                on_left, on_right = pl.ds(e * EXT, WIDE), pl.ds(e * EXT + SUB, WIDE)
                new = wyr[s, i].astype(F32)
                old = wins[s][on_left, :].astype(F32)
                wins[s][on_left, :] = jnp.concatenate([jnp.where(left_side, gap, new), old[8:16]], axis=0).astype(BF16)
                old = wins[s][on_right, :].astype(F32)
                wins[s][on_right, :] = jnp.concatenate([old[0:8], jnp.where(left_side, new, gap)], axis=0).astype(BF16)
            else:
                d, e_in = (1, e) if i < 0 else (0, i - SUB)
                corner = wcr[par, s, d, e_in].astype(F32)
                parts = [jnp.where(left_side, gap, corner), wxr[s, d, e_in].astype(F32), jnp.where(left_side, corner, gap)]
                wins[s][pl.ds(e * EXT, EXT), :] = jnp.concatenate(parts, axis=0).astype(BF16)

    def product(s, pieces):
        for q, part in pieces:
            rows = pl.ds(PIECE * part, PIECE)
            lhs = jnp.concatenate([mat[s, q, t, rows].reshape(PIECE * WIDE, 256) for t in range(TILES)], axis=1)
            out = jnp.dot(lhs, wins[s][...], preferred_element_type=F32)
            cors[s][q, 1 + PIECE * part:1 + PIECE * part + PIECE] = out.reshape(PIECE, WIDE, RHS)

    coefficients(0)
    for q in range(STRIPS):
        f_load(0, q).wait()
    zy_copy(0, 0).wait()
    wait_edges(0, range(STRIPS))
    frame(0, 0, 1.0)
    send_frame(0)
    for work in finish_rows(0, 0, 1.0, None, END_ROWS, True):
        work()
    send_ends(0)

    @pl.loop(MARGIN, SUB - MARGIN, unroll=2)
    def _(i):
        finish_row(0, 0, 1.0, None, i)

    coefficients(1)
    for q in range(STRIPS):
        f_load(1, q).wait()
    zy_copy(1, 0).wait()
    wait_edges(1, (strip_a,))
    frame(1, 0, 1.0)
    send_frame(1)
    send_corners(0, 0)

    def out_store(s, q):
        return pltpu.make_async_copy(apx.at[s, q], out_hbm.at[s, :, q], out_sem.at[s, q])

    def last_update(q):
        @pl.loop(0, SUB, unroll=4)
        def _(i):
            apx[1, q, i] += om_ref[1] * cors[1][q, i + 1]
        out_store(1, q).start()

    def half_sweep(k, s):
        par = k % 2
        more = k < SWEEPS - 1
        first_time = k == 0
        old = 1 - s
        if s == 0:
            old_par = par
            old_live = k >= 0
            scale = jnp.where(first_time, 1.0, om_ref[old])
            gain = jnp.where(first_time, 0.0, om_ref[old])
        else:
            old_par = 1 - par
            old_live = more
            scale = gain = om_ref[old]

        def wait_mat(q):
            @pl.when(first_time)
            def _():
                for t in range(TILES):
                    mat_load(s, q, t).wait()

        @pl.when(old_live)
        def _():
            wait_edges(old, (1, strip_c))

        @pl.when(first_time)
        def _():
            for q in range(STRIPS):
                apx_load(old, q).wait()
        wait_mat(strip_a)
        wy_copy(s, 2).wait()
        wait_x(lambda d: wx_copy(s, d))
        wait_x(lambda d: wc_copy(s, d, par))

        for t in range(TILES):
            fill_tile(s, par, t)
        product(s, ((strip_a, 0), (strip_a, 2), (strip_a, 1), (strip_a, 3)))
        for work in finish_rows(old, old_par, scale, gain, END_ROWS, True):
            work()

        @pl.when(more)
        def _():
            send_zy(s, 1 - par)
            send_zx(s, strip_a)

        @pl.when(old_live)
        def _():
            send_ends(old)

        wait_mat(1)
        wait_mat(strip_c)
        product(s, ((1, 0), (strip_c, 0), (1, 3), (strip_c, 3)))
        for work in finish_rows(old, old_par, scale, gain, list(range(MARGIN, SUB - MARGIN)), False):
            work()

        @pl.when(more)
        def _():
            send_zx(s, 1)
            send_zx(s, strip_c)

        @pl.when(old_live)
        def _():
            send_corners(old, old_par)
        if s == 1:
            @pl.when(jnp.logical_not(more))
            def _():
                for q in range(STRIPS):
                    out_store(old, q).start()
                last_update(strip_a)

        product(s, ((1, 1), (strip_c, 1)))

        @pl.when(more)
        def _():
            zy_copy(s, 1 - par).wait()
            wait_edges(s, (strip_a,))
            frame(s, 1 - par, om_ref[s])
            send_frame(s)
        product(s, ((1, 2), (strip_c, 2)))

    def sweep(k, carry):
        half_sweep(k, 0)
        half_sweep(k, 1)
        return carry

    lax.fori_loop(0, SWEEPS, sweep, 0)
    last_update(1)
    last_update(strip_c)
    for s in range(SYS):
        for q in range(STRIPS):
            out_store(s, q).wait()


def local_solve(forcing, init_guess, cell_coef, solve_rows, relax_factor):
    forcing = forcing.reshape(SYS, SUB, STRIPS, WIDE, RHS)
    init_guess = init_guess.reshape(SYS, SUB, STRIPS, WIDE, RHS)
    mats = solve_rows.reshape(SYS, SUB, STRIPS, WIDE, EXT * EXT)
    hbm = pl.BlockSpec(memory_space=pl.ANY)
    dma = pltpu.SemaphoreType.DMA
    out = pl.pallas_call(
        kernel,
        out_shape=jax.ShapeDtypeStruct((SYS, SUB, STRIPS, WIDE, RHS), F32),
        in_specs=[hbm, hbm, pl.BlockSpec(memory_space=pltpu.VMEM), hbm, pl.BlockSpec(memory_space=pltpu.SMEM)],
        out_specs=hbm,
        scratch_shapes=[
            pltpu.VMEM((SYS, STRIPS, TILES, SUB, WIDE, 256), BF16),
            pltpu.VMEM((SYS, STRIPS, SUB, WIDE, RHS), F32),
            pltpu.VMEM((SYS, STRIPS, SUB, WIDE, RHS), F32),
            pltpu.VMEM((STRIPS, SUB + 2, WIDE, RHS), F32),
            pltpu.VMEM((STRIPS, SUB + 2, WIDE, RHS), F32),
            pltpu.VMEM((EXT * EXT, RHS), BF16),
            pltpu.VMEM((EXT * EXT, RHS), BF16),
            pltpu.VMEM((SYS, STRIPS, SUB + 1, WIDE, LANES), F32),
            pltpu.VMEM((SYS, STRIPS, SUB, WIDE, LANES), F32),
            pltpu.VMEM((SYS, SUB, 1, LANES), F32),
            pltpu.VMEM((SYS, SUB, MARGIN, RHS), BF16),
            pltpu.VMEM((SYS, 2, MARGIN, SUB, RHS), BF16),
            pltpu.VMEM((SYS, SUB, MARGIN, RHS), BF16),
            pltpu.VMEM((SYS, 2, MARGIN, SUB, RHS), BF16),
            pltpu.VMEM((2, SYS, 2, MARGIN, MARGIN, RHS), BF16),
            pltpu.VMEM((SYS, SUB, 1, RHS), F32),
            pltpu.VMEM((2, SYS, SUB, 1, RHS), F32),
            pltpu.VMEM((2, SYS, 8, SUB), F32),
            pltpu.VMEM((SYS, SUB, SUB), F32),
            dma((SYS, STRIPS, TILES)), dma((SYS, STRIPS)), dma((SYS, STRIPS)), dma((SYS, STRIPS)),
            dma((SYS, 3)), dma((SYS, 3)), dma((SYS, 2)), dma((SYS, 2)), dma((2, SYS, 2)), dma((2, SYS, 2)),
            dma((SYS,)), dma((2, SYS)), dma((SYS, 2, STRIPS)), dma((SYS, 2, STRIPS)),
            dma((2,)), dma((2,)), dma(()), dma(()),
        ],
        compiler_params=pltpu.CompilerParams(
            collective_id=0, has_side_effects=True, vmem_limit_bytes=67_043_328),
    )(forcing, init_guess, cell_coef, mats, relax_factor)
    return out.reshape(SYS, SUB, SUB, RHS)


def solution(mesh):
    grid_spec = P(None, "row", "col", None)
    return jax.shard_map(
        local_solve, mesh=mesh,
        in_specs=(grid_spec, grid_spec, P(None, "row", "col"), P(None, "row", "col", None, None), P(None)),
        out_specs=grid_spec, check_vma=False)
```

time: 151 us -> 83.7 us (0.55)
  Pallas kernels: 146 us -> 78.6 us
    pallas_call x1, Pallas kernels: 146 us -> 78.6 us  [local_solve(): pl.pallas_call(kernel, out_shape=jax.ShapeDtypeStruct((SYS, SUB, STRIPS,...]
where the time goes in v2:
time: 83.7 us; the launch traced here: 83.5 us
  Pallas kernels  78.6 us (94%)
  local copies, waits for them, and re-layouts  4.86 us (6%)
    pallas_call x1, Pallas kernels, local_solve(): pl.pallas_call(kernel, out_shape=jax.ShapeDtypeStruct((SYS, SUB, STRIPS,...  78.6 us
    unnamed x1, local copies, waits for them, and re-layouts  4.86 us

profile of v2, /device:TPU:1, one launch (start us, length us, event | category | flops | bytes accessed | tf_op | source)
XLA Modules:
  0.0 83.5 jit_solution(7932086815635614928)
XLA Ops:
  0.0 78.6 %shard_map.55 = f32[2,48,3,16,256]{4,3,2,1,0:T(8,128)} custom-call(f32[2,48,3,16,256]{4,3,2,1,0:T(8,128)} %bitcast.6, f32[2,48,3,16,256]{4,3,2,1,0:T(8,128)} %bitcast.7, f32[2,48,48]{2,1,0:T(8,128)} %c_ref.1, bf16[2,48,3,16,4096]{4,3,2,1,0:T(8,128)(2,1)} %bitcast.4, f32[2]{0:T(128)} %om_ref.1), custom_call_target="tpu_custom_call" | custom-call | tf_op jit(solution)/shard_map/pallas_call | solution.py:452
  78.6 4.9 %copy.7 = f32[2,48,48,256]{3,2,1,0:T(8,128)} copy(f32[2,48,48,256]{3,2,1,0:T(8,128)} %bitcast.5) | data formatting | bytes 9437184

commit v3 on v2

--- a/solution.py
+++ b/solution.py
@@ -15,6 +15,7 @@
 WIDE = 16
 LANES = 128
 PIECE = 12
+EARLY = 20
 TILES = 16
 F32 = jnp.float32
 BF16 = jnp.bfloat16
@@ -32,9 +33,9 @@
     return pltpu.roll(values, values.shape[0] - 1, 0)
 
 
-def kernel(f_hbm, u0_hbm, c_ref, s_hbm, om_ref, out_hbm,
-           mat, res, apx, cor0, cor1, win0, win1, fx, fy, fyr,
-           wys, wxs, wyr, wxr, wcr, zys, zyr, cxr, cyr,
+def kernel(f_hbm, u0_hbm, c_ref, s_hbm, om_ref, apx,
+           mat, res, cor0, cor1, win0, win1, fx, fy, fyr,
+           wys, wxs, wyr, wxr, wcr, zys, zyr, cxr, cys, cyr, cyb,
            mat_sem, u_sem, f_sem, out_sem,
            wy_ss, wy_rs, wx_ss, wx_rs, wc_ss, wc_rs,
            zy_ss, zy_rs, zx_ss, zx_rs, cx_ss, cx_rs, cy_ss, cy_rs):
@@ -60,12 +61,14 @@
     def zy_copy(s, par):
         return remote(zys.at[s], zyr.at[par, s], zy_ss.at[s], zy_rs.at[par, s], 0, 1)
 
-    def zx_copy(s, d, q):
+    def zx_copy(s, d, part):
+        strips_of = (pl.ds(strip_a, 1), pl.ds(col, 2))[part]
         start, land = ((1, SUB + 1), (SUB, 0))[d]
-        return remote(cors[s].at[q, start], cors[s].at[q, land], zx_ss.at[s, d, q], zx_rs.at[s, d, q], steps[d], 0)
+        return remote(cors[s].at[strips_of, start], cors[s].at[strips_of, land],
+                      zx_ss.at[s, d, part], zx_rs.at[s, d, part], steps[d], 0)
 
     def wy_copy(s, part):
-        rows = pl.ds(*((0, MARGIN), (SUB - MARGIN, MARGIN), (MARGIN, SUB - 2 * MARGIN))[part])
+        rows = pl.ds(*((0, MARGIN), (SUB - MARGIN, MARGIN), (MARGIN, EARLY), (MARGIN + EARLY, SUB - 2 * MARGIN - EARLY))[part])
         return remote(wys.at[s, rows], wyr.at[s, rows], wy_ss.at[s, part], wy_rs.at[s, part], 0, 1)
 
     def wx_copy(s, d):
@@ -80,23 +83,15 @@
         return remote(c_ref.at[:, pl.ds(first, 8), :], cxr.at[d], cx_ss.at[d], cx_rs.at[d], steps[d], 0)
 
     def cy_copy():
-        return remote(c_ref, cyr, cy_ss, cy_rs, 0, 1)
-
-    def start_x(make):
+        return remote(cys, cyr, cy_ss, cy_rs, 0, 1)
+
+    def with_rows(work, cond=None):
         for d in range(2):
-            @pl.when(has_nb[d])
-            def _():
-                make(d).start()
-
-    def wait_x(make):
-        for d in range(2):
-            @pl.when(has_nb[d])
-            def _():
-                make(d).wait_send()
-
-            @pl.when(has_nb[1 - d])
-            def _():
-                make(d).wait_recv()
+            pl.when(has_nb[d] if cond is None else jnp.logical_and(has_nb[d], cond))(lambda d=d: work(d))
+
+    def settle(make, d):
+        make(d).wait_send()
+        make(1 - d).wait_recv()
 
     for s in range(SYS):
         for q in range(STRIPS):
@@ -127,9 +122,9 @@
         return pltpu.make_async_copy(s_hbm.at[s, :, q, :, pl.ds(256 * t, 256)], mat.at[s, q, t], mat_sem.at[s, q, t])
 
     order = (strip_a, 1, strip_c)
-    for load in (u_load, f_load):
-        for s in range(SYS):
-            for q in range(STRIPS):
+    for s in range(SYS):
+        for load in (u_load, f_load):
+            for q in order:
                 load(s, q).start()
     for q in order:
         for t in range(TILES):
@@ -157,9 +152,17 @@
                     for par in range(2):
                         wcr[par, s, d, e] = jnp.zeros((MARGIN, RHS), BF16)
 
+    eye = (lax.broadcasted_iota(jnp.int32, (SUB, SUB), 0) == lax.broadcasted_iota(jnp.int32, (SUB, SUB), 1)).astype(F32)
+    lane = lax.broadcasted_iota(jnp.int32, (1, SUB), 1)
+    mine = (lane == jnp.where(left_side, SUB - 1, 0)).astype(F32)
+    for s in range(SYS):
+        column = jnp.sum(c_ref[s] * mine, axis=1, keepdims=True)
+        line = jnp.sum(jnp.broadcast_to(column, (SUB, SUB)) * eye, axis=0, keepdims=True)
+        cys[s] = jnp.broadcast_to(line, (8, SUB))
+
     pl.semaphore_wait(barrier, 1 + has_up.astype(jnp.int32) + has_dn.astype(jnp.int32))
     cy_copy().start()
-    start_x(cx_copy)
+    with_rows(lambda d: cx_copy(d).start())
 
     def send_zy(s, par):
         @pl.loop(0, SUB, unroll=8)
@@ -168,32 +171,28 @@
             zys[s, i] = jnp.where(left_side, tile[7:8], tile[0:1])
         zy_copy(s, par).start()
 
-    def send_zx(s, q):
-        start_x(lambda d: zx_copy(s, d, q))
-
     for s in range(SYS):
-        for q in range(STRIPS):
+        u_load(s, strip_a).wait()
+        send_zy(s, 0)
+        for q in (1, strip_c):
             u_load(s, q).wait()
-        send_zy(s, 0)
-        for q in range(STRIPS):
-            send_zx(s, q)
+        with_rows(lambda d: [zx_copy(s, d, part).start() for part in range(2)] and None)
 
     cy_copy().wait()
-    wait_x(cx_copy)
-    eye = (lax.broadcasted_iota(jnp.int32, (SUB, SUB), 0) == lax.broadcasted_iota(jnp.int32, (SUB, SUB), 1)).astype(F32)
-    lane = lax.broadcasted_iota(jnp.int32, (1, SUB), 1)
-    near = (lane == jnp.where(left_side, 0, SUB - 1)).astype(F32)
+    with_rows(lambda d: settle(cx_copy, d))
 
     def spread(line):
         cells = jnp.sum(jnp.broadcast_to(line, (SUB, SUB)) * eye, axis=1, keepdims=True)
         return jnp.broadcast_to(cells, (SUB, LANES))
 
     def coefficients(s):
+        cyb[...] = spread(cyr[s, 0:1, :])
+
         def one_row(i, before):
             line = c_ref[s, pl.ds(i, 1), :]
             here = spread(line)
             face = 0.5 * (before + here)
-            other = jnp.broadcast_to(jnp.sum(cyr[s, pl.ds(i, 1), :] * near, axis=1, keepdims=True), (8, LANES))
+            other = jnp.broadcast_to(cyb[pl.ds(i, 1), :], (8, LANES))
             first = jnp.broadcast_to(here[0:1], (8, LANES))
             last = jnp.broadcast_to(here[SUB - 1:SUB], (8, LANES))
             beyond = jnp.where(left_side, first, other)
@@ -239,10 +238,12 @@
         for part in range(3):
             wy_copy(s, part).start()
 
-    def send_corners(s, par):
+    def send_rest(s):
+        wy_copy(s, 3).start()
+
+    def wait_corners(s):
         for part in range(2):
             wy_copy(s, part).wait()
-        start_x(lambda d: wc_copy(s, d, par))
 
     def strips(ref, i):
         return jnp.concatenate([ref[q, i] for q in range(STRIPS)], axis=0)
@@ -286,12 +287,8 @@
 
     END_ROWS = list(range(MARGIN)) + list(range(SUB - MARGIN, SUB))
 
-    def send_ends(s):
-        start_x(lambda d: wx_copy(s, d))
-
-    def wait_edges(s, which):
-        for q in which:
-            wait_x(lambda d: zx_copy(s, d, q))
+    def edges(s, part):
+        return lambda d: settle(lambda way: zx_copy(s, way, part), d)
 
     def fill_tile(s, par, t):
         gap = jnp.zeros((MARGIN, RHS), F32)
@@ -310,23 +307,42 @@
                 parts = [jnp.where(left_side, gap, corner), wxr[s, d, e_in].astype(F32), jnp.where(left_side, corner, gap)]
                 wins[s][pl.ds(e * EXT, EXT), :] = jnp.concatenate(parts, axis=0).astype(BF16)
 
-    def product(s, pieces):
-        for q, part in pieces:
-            rows = pl.ds(PIECE * part, PIECE)
-            lhs = jnp.concatenate([mat[s, q, t, rows].reshape(PIECE * WIDE, 256) for t in range(TILES)], axis=1)
-            out = jnp.dot(lhs, wins[s][...], preferred_element_type=F32)
-            cors[s][q, 1 + PIECE * part:1 + PIECE * part + PIECE] = out.reshape(PIECE, WIDE, RHS)
+    def product(s, units, works=(), fill=None):
+        sums = [None] * len(units)
+        done = 0
+        for t in range(TILES):
+            if fill is not None:
+                for ahead in ((0, 1, 2) if t == 0 else (t + 2,)):
+                    if ahead < TILES:
+                        fill(ahead)
+            window = wins[s][256 * t:256 * (t + 1), :]
+            for m, pieces in enumerate(units):
+                lhs = [mat[s, q, t, pl.ds(PIECE * part, PIECE)].reshape(PIECE * WIDE, 256) for q, part in pieces]
+                term = jnp.dot(jnp.concatenate(lhs, axis=0), window, preferred_element_type=F32)
+                sums[m] = term if sums[m] is None else sums[m] + term
+            upto = len(works) * (t + 1) // (TILES + 1)
+            for work in works[done:upto]:
+                work()
+            done = upto
+        for work in works[done:]:
+            work()
+        for m, pieces in enumerate(units):
+            for n, (q, part) in enumerate(pieces):
+                rows = slice(PIECE * WIDE * n, PIECE * WIDE * (n + 1))
+                cors[s][q, 1 + PIECE * part:1 + PIECE * part + PIECE] = sums[m][rows].reshape(PIECE, WIDE, RHS)
 
     coefficients(0)
     for q in range(STRIPS):
         f_load(0, q).wait()
     zy_copy(0, 0).wait()
-    wait_edges(0, range(STRIPS))
+    with_rows(edges(0, 0))
     frame(0, 0, 1.0)
     send_frame(0)
+    send_rest(0)
+    with_rows(edges(0, 1))
     for work in finish_rows(0, 0, 1.0, None, END_ROWS, True):
         work()
-    send_ends(0)
+    with_rows(lambda d: wx_copy(0, d).start())
 
     @pl.loop(MARGIN, SUB - MARGIN, unroll=2)
     def _(i):
@@ -336,19 +352,16 @@
     for q in range(STRIPS):
         f_load(1, q).wait()
     zy_copy(1, 0).wait()
-    wait_edges(1, (strip_a,))
+    with_rows(edges(1, 0))
     frame(1, 0, 1.0)
     send_frame(1)
-    send_corners(0, 0)
-
-    def out_store(s, q):
-        return pltpu.make_async_copy(apx.at[s, q], out_hbm.at[s, :, q], out_sem.at[s, q])
+    wait_corners(0)
+    with_rows(lambda d: wc_copy(0, d, 0).start())
 
     def last_update(q):
         @pl.loop(0, SUB, unroll=4)
         def _(i):
             apx[1, q, i] += om_ref[1] * cors[1][q, i + 1]
-        out_store(1, q).start()
 
     def half_sweep(k, s):
         par = k % 2
@@ -357,7 +370,7 @@
         old = 1 - s
         if s == 0:
             old_par = par
-            old_live = k >= 0
+            old_live = None
             scale = jnp.where(first_time, 1.0, om_ref[old])
             gain = jnp.where(first_time, 0.0, om_ref[old])
         else:
@@ -365,70 +378,64 @@
             old_live = more
             scale = gain = om_ref[old]
 
-        def wait_mat(q):
-            @pl.when(first_time)
-            def _():
+        def when_old(work):
+            if old_live is None:
+                work()
+            else:
+                pl.when(old_live)(work)
+
+        def frame_parts(d):
+            settle(lambda way: wx_copy(s, way), d)
+            settle(lambda way: wc_copy(s, way, par), d)
+
+        @pl.when(first_time)
+        def _():
+            for q in range(STRIPS):
+                apx_load(old, q).wait()
+            for t in range(TILES):
+                mat_load(s, strip_a, t).wait()
+        for part in (2, 3):
+            wy_copy(s, part).wait()
+        with_rows(frame_parts)
+
+        product(s, (((strip_a, 0), (strip_a, 1)), ((strip_a, 2), (strip_a, 3))),
+                finish_rows(old, old_par, scale, gain, END_ROWS[1:-1], True), lambda t: fill_tile(s, par, t))
+
+        @pl.when(more)
+        def _():
+            send_zy(s, 1 - par)
+        with_rows(lambda d: zx_copy(s, d, 0).start(), more)
+        when_old(lambda: wy_copy(old, 3).start())
+        with_rows(edges(old, 1), old_live)
+        for work in finish_rows(old, old_par, scale, gain, END_ROWS[:1] + END_ROWS[-1:], True):
+            work()
+        with_rows(lambda d: wx_copy(old, d).start(), old_live)
+
+        @pl.when(first_time)
+        def _():
+            for q in (1, strip_c):
                 for t in range(TILES):
                     mat_load(s, q, t).wait()
-
-        @pl.when(old_live)
-        def _():
-            wait_edges(old, (1, strip_c))
-
-        @pl.when(first_time)
-        def _():
-            for q in range(STRIPS):
-                apx_load(old, q).wait()
-        wait_mat(strip_a)
-        wy_copy(s, 2).wait()
-        wait_x(lambda d: wx_copy(s, d))
-        wait_x(lambda d: wc_copy(s, d, par))
-
-        for t in range(TILES):
-            fill_tile(s, par, t)
-        product(s, ((strip_a, 0), (strip_a, 2), (strip_a, 1), (strip_a, 3)))
-        for work in finish_rows(old, old_par, scale, gain, END_ROWS, True):
-            work()
-
-        @pl.when(more)
-        def _():
-            send_zy(s, 1 - par)
-            send_zx(s, strip_a)
-
-        @pl.when(old_live)
-        def _():
-            send_ends(old)
-
-        wait_mat(1)
-        wait_mat(strip_c)
-        product(s, ((1, 0), (strip_c, 0), (1, 3), (strip_c, 3)))
-        for work in finish_rows(old, old_par, scale, gain, list(range(MARGIN, SUB - MARGIN)), False):
-            work()
-
-        @pl.when(more)
-        def _():
-            send_zx(s, 1)
-            send_zx(s, strip_c)
-
-        @pl.when(old_live)
-        def _():
-            send_corners(old, old_par)
+        product(s, (((1, 0), (strip_c, 0)), ((1, 3), (strip_c, 3))),
+                finish_rows(old, old_par, scale, gain, list(range(MARGIN, SUB - MARGIN - 6)), False))
+        with_rows(lambda d: zx_copy(s, d, 1).start(), more)
+        when_old(lambda: wait_corners(old))
+        with_rows(lambda d: wc_copy(old, d, old_par).start(), old_live)
+
+        product(s, (((1, 1),), ((strip_c, 1),)),
+                finish_rows(old, old_par, scale, gain, list(range(SUB - MARGIN - 6, SUB - MARGIN)), False))
         if s == 1:
             @pl.when(jnp.logical_not(more))
             def _():
-                for q in range(STRIPS):
-                    out_store(old, q).start()
                 last_update(strip_a)
 
-        product(s, ((1, 1), (strip_c, 1)))
-
         @pl.when(more)
         def _():
             zy_copy(s, 1 - par).wait()
-            wait_edges(s, (strip_a,))
+            with_rows(edges(s, 0))
             frame(s, 1 - par, om_ref[s])
             send_frame(s)
-        product(s, ((1, 2), (strip_c, 2)))
+        product(s, (((1, 2),), ((strip_c, 2),)))
 
     def sweep(k, carry):
         half_sweep(k, 0)
@@ -438,9 +445,6 @@
     lax.fori_loop(0, SWEEPS, sweep, 0)
     last_update(1)
     last_update(strip_c)
-    for s in range(SYS):
-        for q in range(STRIPS):
-            out_store(s, q).wait()
 
 
 def local_solve(forcing, init_guess, cell_coef, solve_rows, relax_factor):
@@ -451,12 +455,11 @@
     dma = pltpu.SemaphoreType.DMA
     out = pl.pallas_call(
         kernel,
-        out_shape=jax.ShapeDtypeStruct((SYS, SUB, STRIPS, WIDE, RHS), F32),
+        out_shape=pltpu.VMEM((SYS, STRIPS, SUB, WIDE, RHS), F32),
         in_specs=[hbm, hbm, pl.BlockSpec(memory_space=pltpu.VMEM), hbm, pl.BlockSpec(memory_space=pltpu.SMEM)],
-        out_specs=hbm,
+        out_specs=pl.BlockSpec(memory_space=pltpu.VMEM),
         scratch_shapes=[
             pltpu.VMEM((SYS, STRIPS, TILES, SUB, WIDE, 256), BF16),
-            pltpu.VMEM((SYS, STRIPS, SUB, WIDE, RHS), F32),
             pltpu.VMEM((SYS, STRIPS, SUB, WIDE, RHS), F32),
             pltpu.VMEM((STRIPS, SUB + 2, WIDE, RHS), F32),
             pltpu.VMEM((STRIPS, SUB + 2, WIDE, RHS), F32),
@@ -473,16 +476,18 @@
             pltpu.VMEM((SYS, SUB, 1, RHS), F32),
             pltpu.VMEM((2, SYS, SUB, 1, RHS), F32),
             pltpu.VMEM((2, SYS, 8, SUB), F32),
-            pltpu.VMEM((SYS, SUB, SUB), F32),
+            pltpu.VMEM((SYS, 8, SUB), F32),
+            pltpu.VMEM((SYS, 8, SUB), F32),
+            pltpu.VMEM((SUB, LANES), F32),
             dma((SYS, STRIPS, TILES)), dma((SYS, STRIPS)), dma((SYS, STRIPS)), dma((SYS, STRIPS)),
-            dma((SYS, 3)), dma((SYS, 3)), dma((SYS, 2)), dma((SYS, 2)), dma((2, SYS, 2)), dma((2, SYS, 2)),
-            dma((SYS,)), dma((2, SYS)), dma((SYS, 2, STRIPS)), dma((SYS, 2, STRIPS)),
+            dma((SYS, 4)), dma((SYS, 4)), dma((SYS, 2)), dma((SYS, 2)), dma((2, SYS, 2)), dma((2, SYS, 2)),
+            dma((SYS,)), dma((2, SYS)), dma((SYS, 2, 2)), dma((SYS, 2, 2)),
             dma((2,)), dma((2,)), dma(()), dma(()),
         ],
         compiler_params=pltpu.CompilerParams(
-            collective_id=0, has_side_effects=True, vmem_limit_bytes=67_043_328),
+            collective_id=0, has_side_effects=True, vmem_limit_bytes=62_000_000),
     )(forcing, init_guess, cell_coef, mats, relax_factor)
-    return out.reshape(SYS, SUB, SUB, RHS)
+    return out.transpose(0, 2, 1, 3, 4).reshape(SYS, SUB, SUB, RHS)
 
 
 def solution(mesh):

time: 83.7 us -> 78.3 us (0.935)
  Pallas kernels: 78.6 us -> 75.5 us
  local copies, waits for them, and re-layouts: 4.86 us -> 2.69 us
    unnamed x1 -> x0, local copies, waits for them, and re-layouts: 4.86 us -> none
    pallas_call x1, Pallas kernels: 78.6 us -> 75.5 us  [local_solve(): pl.pallas_call(kernel, out_shape=pltpu.VMEM((SYS, STRIPS, SUB, WIDE, RHS)...]
    transpose x0 -> x1, local copies, waits for them, and re-layouts: none -> 2.69 us  [local_solve(): return out.transpose(0, 2, 1, 3, 4).reshape(SYS, SUB, SUB, RHS)]
where the time goes in v3:
time: 78.3 us; the launch traced here: 78.2 us
  Pallas kernels  75.5 us (96%)
  local copies, waits for them, and re-layouts  2.69 us (3%)
    pallas_call x1, Pallas kernels, local_solve(): pl.pallas_call(kernel, out_shape=pltpu.VMEM((SYS, STRIPS, SUB, WIDE, RHS)...  75.5 us
    transpose x1, local copies, waits for them, and re-layouts, local_solve(): return out.transpose(0, 2, 1, 3, 4).reshape(SYS, SUB, SUB, RHS)  2.69 us

profile of v3, /device:TPU:1, one launch (start us, length us, event | category | flops | bytes accessed | tf_op | source)
XLA Modules:
  0.0 78.2 jit_solution(17156845206020592907)
XLA Ops:
  0.0 75.5 %shard_map.55 = f32[2,3,48,16,256]{4,3,2,1,0:T(8,128)S(1)} custom-call(f32[2,48,3,16,256]{4,3,2,1,0:T(8,128)} %bitcast.7, f32[2,48,3,16,256]{4,3,2,1,0:T(8,128)} %bitcast.8, f32[2,48,48]{2,1,0:T(8,128)} %c_ref.1, bf16[2,48,3,16,4096]{4,3,2,1,0:T(8,128)(2,1)} %bitcast.6, f32[2]{0:T(128)} %om_ref.1), custom_call_target="tpu_custom_call" | custom-call | tf_op jit(solution)/shard_map/pallas_call | solution.py:456
  75.5 2.7 %copy.6 = f32[2,48,3,16,256]{4,3,2,1,0:T(8,128)} copy(f32[2,48,3,16,256]{4,3,1,2,0:T(8,128)S(1)} %bitcast.5) | data formatting | bytes 9437184 | tf_op jit(solution)/shard_map/transpose | solution.py:490

commit v4 on v3

--- a/solution.py
+++ b/solution.py
@@ -16,6 +16,7 @@
 LANES = 128
 PIECE = 12
 EARLY = 20
+IN_FIRST, IN_SECOND, IN_THIRD = 0, 16, 16
 TILES = 16
 F32 = jnp.float32
 BF16 = jnp.bfloat16
@@ -307,20 +308,16 @@
                 parts = [jnp.where(left_side, gap, corner), wxr[s, d, e_in].astype(F32), jnp.where(left_side, corner, gap)]
                 wins[s][pl.ds(e * EXT, EXT), :] = jnp.concatenate(parts, axis=0).astype(BF16)
 
-    def product(s, units, works=(), fill=None):
+    def product(s, units, works=(), order=range(TILES)):
         sums = [None] * len(units)
         done = 0
-        for t in range(TILES):
-            if fill is not None:
-                for ahead in ((0, 1, 2) if t == 0 else (t + 2,)):
-                    if ahead < TILES:
-                        fill(ahead)
+        for step, t in enumerate(order):
             window = wins[s][256 * t:256 * (t + 1), :]
             for m, pieces in enumerate(units):
                 lhs = [mat[s, q, t, pl.ds(PIECE * part, PIECE)].reshape(PIECE * WIDE, 256) for q, part in pieces]
                 term = jnp.dot(jnp.concatenate(lhs, axis=0), window, preferred_element_type=F32)
                 sums[m] = term if sums[m] is None else sums[m] + term
-            upto = len(works) * (t + 1) // (TILES + 1)
+            upto = len(works) * (step + 1) // (TILES + 1)
             for work in works[done:upto]:
                 work()
             done = upto
@@ -355,6 +352,10 @@
     with_rows(edges(1, 0))
     frame(1, 0, 1.0)
     send_frame(1)
+    with_rows(edges(1, 1))
+    for work in finish_rows(1, 0, 1.0, None, END_ROWS, True):
+        work()
+    with_rows(lambda d: wx_copy(1, d).start())
     wait_corners(0)
     with_rows(lambda d: wc_copy(0, d, 0).start())
 
@@ -384,32 +385,38 @@
             else:
                 pl.when(old_live)(work)
 
+        def middle(skip, count):
+            first = MARGIN + skip
+            return finish_rows(old, old_par, scale, gain, list(range(first, first + count)), False)
+
         def frame_parts(d):
             settle(lambda way: wx_copy(s, way), d)
             settle(lambda way: wc_copy(s, way, par), d)
 
         @pl.when(first_time)
         def _():
-            for q in range(STRIPS):
-                apx_load(old, q).wait()
+            for q in range(STRIPS if s == 0 else 0):
+                apx_load(1, q).wait()
+                apx_load(0, q).wait()
             for t in range(TILES):
                 mat_load(s, strip_a, t).wait()
         for part in (2, 3):
             wy_copy(s, part).wait()
+        for t in range(2, TILES - 2):
+            fill_tile(s, par, t)
         with_rows(frame_parts)
+        late = (0, 1, TILES - 2, TILES - 1)
+        for t in late:
+            fill_tile(s, par, t)
 
         product(s, (((strip_a, 0), (strip_a, 1)), ((strip_a, 2), (strip_a, 3))),
-                finish_rows(old, old_par, scale, gain, END_ROWS[1:-1], True), lambda t: fill_tile(s, par, t))
+                middle(0, IN_FIRST), tuple(range(2, TILES - 2)) + late)
 
         @pl.when(more)
         def _():
             send_zy(s, 1 - par)
         with_rows(lambda d: zx_copy(s, d, 0).start(), more)
         when_old(lambda: wy_copy(old, 3).start())
-        with_rows(edges(old, 1), old_live)
-        for work in finish_rows(old, old_par, scale, gain, END_ROWS[:1] + END_ROWS[-1:], True):
-            work()
-        with_rows(lambda d: wx_copy(old, d).start(), old_live)
 
         @pl.when(first_time)
         def _():
@@ -417,13 +424,13 @@
                 for t in range(TILES):
                     mat_load(s, q, t).wait()
         product(s, (((1, 0), (strip_c, 0)), ((1, 3), (strip_c, 3))),
-                finish_rows(old, old_par, scale, gain, list(range(MARGIN, SUB - MARGIN - 6)), False))
+                middle(IN_FIRST, IN_SECOND))
         with_rows(lambda d: zx_copy(s, d, 1).start(), more)
         when_old(lambda: wait_corners(old))
         with_rows(lambda d: wc_copy(old, d, old_par).start(), old_live)
 
-        product(s, (((1, 1),), ((strip_c, 1),)),
-                finish_rows(old, old_par, scale, gain, list(range(SUB - MARGIN - 6, SUB - MARGIN)), False))
+        product(s, (((1, 1), (1, 2)), ((strip_c, 1), (strip_c, 2))),
+                middle(IN_FIRST + IN_SECOND, IN_THIRD))
         if s == 1:
             @pl.when(jnp.logical_not(more))
             def _():
@@ -435,7 +442,19 @@
             with_rows(edges(s, 0))
             frame(s, 1 - par, om_ref[s])
             send_frame(s)
-        product(s, (((1, 2),), ((strip_c, 2),)))
+            with_rows(edges(s, 1))
+            for work in finish_rows(s, 1 - par, om_ref[s], om_ref[s], END_ROWS, True):
+                work()
+            with_rows(lambda d: wx_copy(s, d).start())
+
+        if s == 0:
+            @pl.when(jnp.logical_not(more))
+            def _():
+                for q in range(STRIPS):
+                    for first in (0, SUB - MARGIN):
+                        @pl.loop(first, first + MARGIN, unroll=4)
+                        def _(i):
+                            apx[0, q, i] += om_ref[0] * cors[0][q, i + 1]
 
     def sweep(k, carry):
         half_sweep(k, 0)

time: 78.3 us -> 75 us (0.958)
  Pallas kernels: 75.5 us -> 72.1 us
    pallas_call x1, Pallas kernels: 75.5 us -> 72.1 us  [local_solve(): pl.pallas_call(kernel, out_shape=pltpu.VMEM((SYS, STRIPS, SUB, WIDE, RHS)...]
where the time goes in v4:
time: 75 us; the launch traced here: 74.8 us
  Pallas kernels  72.1 us (96%)
  local copies, waits for them, and re-layouts  2.69 us (4%)
    pallas_call x1, Pallas kernels, local_solve(): pl.pallas_call(kernel, out_shape=pltpu.VMEM((SYS, STRIPS, SUB, WIDE, RHS)...  72.1 us
    transpose x1, local copies, waits for them, and re-layouts, local_solve(): return out.transpose(0, 2, 1, 3, 4).reshape(SYS, SUB, SUB, RHS)  2.69 us

profile of v4, /device:TPU:1, one launch (start us, length us, event | category | flops | bytes accessed | tf_op | source)
XLA Modules:
  0.0 74.8 jit_solution(6770935275985526882)
XLA Ops:
  0.0 72.1 %shard_map.55 = f32[2,3,48,16,256]{4,3,2,1,0:T(8,128)S(1)} custom-call(f32[2,48,3,16,256]{4,3,2,1,0:T(8,128)} %bitcast.7, f32[2,48,3,16,256]{4,3,2,1,0:T(8,128)} %bitcast.8, f32[2,48,48]{2,1,0:T(8,128)} %c_ref.1, bf16[2,48,3,16,4096]{4,3,2,1,0:T(8,128)(2,1)} %bitcast.6, f32[2]{0:T(128)} %om_ref.1), custom_call_target="tpu_custom_call" | custom-call | tf_op jit(solution)/shard_map/pallas_call | solution.py:475
  72.1 2.7 %copy.6 = f32[2,48,3,16,256]{4,3,2,1,0:T(8,128)} copy(f32[2,48,3,16,256]{4,3,1,2,0:T(8,128)S(1)} %bitcast.5) | data formatting | bytes 9437184 | tf_op jit(solution)/shard_map/transpose | solution.py:509
